TPU v7x, 512 devices: a whole 4x4x16 slice. The times are simulated.
512 devices in a mesh: space: 64 (over z, x_lo, core), shot: 8 (over x_hi, y).
Axes of the slice: x: 4 (x_hi: 2, x_lo: 2; x = x_hi * 2 + x_lo), y: 4, z: 16, core: 2. Of those that a mesh axis runs over, the one named last changes fastest.
Arguments:
- courant: float32 [1024, 64, 128], P('space'), may hold values from 0.15 to 0.42
- p_current: float32 [8, 1024, 64, 128], P('shot', 'space'), may hold values from -6 to 6
- p_later: float32 [8, 1024, 64, 128], P('shot', 'space'), may hold values from -6 to 6
- q_current: float32 [8, 1024, 64, 128], P('shot', 'space'), may hold values from -6 to 6
- q_later: float32 [8, 1024, 64, 128], P('shot', 'space'), may hold values from -6 to 6
- wavelet: float32 [8, 6], P('shot'), may hold values from -24 to 24
- source_cell: int32 [8], P('shot'), may hold values from 0 to 8388607
- receiver_cells: int32 [8, 256], P('shot'), may hold values from 0 to 8388607
- residual_data: float32 [8, 6, 256], P('shot'), may hold values from -6 to 6
Outputs:
- gradient: float32 [1024, 64, 128], P('space', 'shot')
- q_final: float32 [8, 1024, 64, 128], P('shot', 'space')
Inputs may be any that keep to these rules, and one draw needn't show every extreme that they name: `source_cell`: a flat cell index of the whole grid. `receiver_cells`: flat cell indices of the whole grid; cells may repeat.
All inputs are finite; a program needn't handle non-finite values.
Results may differ from a plain program's by a relative error of at most 0.0003.
Values sent between devices are 32-bit elements; how exact they have to be, the bound alone decides.
No kernel may reach another device: no remote copies, remote signals or barrier semaphores. Data moves between devices by JAX's collectives and lax.ppermute only.
A program may use at most 64 MiB of HBM per device.

v0:
```python
import jax
import jax.numpy as jnp
from jax import lax
from jax.sharding import PartitionSpec as P

STEPS = 6


coefs = (-205.0 / 72.0, 8.0 / 5.0, -1.0 / 5.0, 8.0 / 315.0, -1.0 / 560.0)


def extended(value, sides, width):
    for axis, dim in sides:
        count, length = (lax.axis_size(axis), value.shape[dim])
        up = [(i, (i + 1) % count) for i in range(count - 1)]
        down = [(j, i) for i, j in up]
        last = lax.slice_in_dim(value, length - width, length, axis=dim)
        leading = lax.slice_in_dim(value, 0, width, axis=dim)
        before = lax.ppermute(last, axis, up)
        after = lax.ppermute(leading, axis, down)
        value = jnp.concatenate([before, value, after], axis=dim)
    return value


def split_up(value, dim, count):
    dims = value.shape
    blocks = value.reshape(*dims[:dim], count, dims[dim] // count, *dims[dim + 1 :])
    return jnp.moveaxis(blocks, dim, 0)


def sum_at_owner(value, axis, dim):
    blocks = split_up(value, dim, lax.axis_size(axis))
    arrived = lax.all_to_all(blocks, axis, split_axis=0, concat_axis=0, tiled=True)
    return arrived.sum(axis=0)


def laplace_rows(field):
    extent = field.shape[0]
    core = field[4 : extent - 4]
    total = 3.0 * coefs[0] * core
    for j in range(1, 5):
        total = total + coefs[j] * (field[4 + j : extent - 4 + j] + field[4 - j : extent - 4 - j])
    width_y = core.shape[1]
    padded_y = jnp.pad(core, ((0, 0), (4, 4), (0, 0)))
    for j in range(1, 5):
        total = total + coefs[j] * (
            padded_y[:, 4 + j : 4 + j + width_y] + padded_y[:, 4 - j : 4 - j + width_y]
        )
    width_z = core.shape[2]
    padded_z = jnp.pad(core, ((0, 0), (0, 0), (4, 4)))
    for j in range(1, 5):
        total = total + coefs[j] * (
            padded_z[:, :, 4 + j : 4 + j + width_z] + padded_z[:, :, 4 - j : 4 - j + width_z]
        )
    return total


def inject_local(field, first_row, cells, values):
    flat = field.reshape(-1)
    plane = field.shape[1] * field.shape[2]
    local = cells - first_row * plane
    inside = (local >= 0) & (local < flat.shape[0])
    flat = flat.at[jnp.where(inside, local, 0)].add(jnp.where(inside, values, 0.0))
    return flat.reshape(field.shape)


def body(
    courant,
    p_current,
    p_later,
    q_current,
    q_later,
    wavelet,
    source_cell,
    receiver_cells,
    residual_data,
):
    rows = courant.shape[0]
    first = lax.axis_index("space") * rows
    speed2 = courant * courant
    pc, pn, qc, qn = (p_current[0], p_later[0], q_current[0], q_later[0])
    wave = wavelet[0]
    receivers = receiver_cells[0]
    residual = residual_data[0]
    grad = jnp.zeros(pc.shape, jnp.float32)
    for k in range(STEPS):
        both = extended(jnp.stack((pc, qc)), (("space", 1),), 4)
        p_wide, q_wide = (both[0], both[1])
        lp = laplace_rows(p_wide)
        lq = laplace_rows(q_wide)
        grad = grad + qc * lp
        p_new = inject_local(2.0 * pc - pn + speed2 * lp, first, source_cell, wave[k][None])
        q_new = inject_local(2.0 * qc - qn + speed2 * lq, first, receivers, residual[k])
        pn, pc = (pc, p_new)
        qn, qc = (qc, q_new)
    summed = sum_at_owner(grad, "shot", 1)
    gradient = summed * (1.0 / (STEPS * lax.axis_size("shot")))
    return (gradient, qc[None])


def solution(mesh):
    in_specs = (
        P("space", None, None),
        P("shot", "space", None, None),
        P("shot", "space", None, None),
        P("shot", "space", None, None),
        P("shot", "space", None, None),
        P("shot", None),
        P("shot"),
        P("shot", None),
        P("shot", None, None),
    )
    out_specs = (P("space", "shot", None), P("shot", "space", None, None))
    return jax.shard_map(body, mesh=mesh, in_specs=in_specs, out_specs=out_specs, check_vma=False)
```

profile of v0, /device:TPU:384, one launch (start us, length us, event | category | flops | bytes accessed | tf_op | source)
XLA Modules:
  0.0 141.4 jit_solution(12977867723830938232)
XLA Ops:
  2.7 4.6 %collective-permute-start = (f32[2,4,64,128]{3,2,1,0:T(8,128)}, f32[2,4,64,128]{3,2,1,0:T(8,128)S(1)}, u32[]{:S(2)}, u32[]{:S(2)}) collective-permute-start(f32[2,4,64,128]{3,2,1,0:T(8,128)} %get-tuple-element.92), channel_id=1, source_target_pairs={{8,0},{16,8},{24,16},{32,24},{40,32},{48,40},{56,48},{64,56},{72,6... | collective-permute-start | bytes 786440 | tf_op jit(solution)/shard_map/ppermute | solution.py:20
  11.5 5.6 %collective-permute-done.1 = f32[2,4,64,128]{3,2,1,0:T(8,128)S(1)} collective-permute-done((f32[2,4,64,128]{3,2,1,0:T(8,128)S(1)}, f32[2,4,64,128]{3,2,1,0:T(8,128)S(1)}, u32[]{:S(2)}, u32[]{:S(2)}) %collective-permute-start.1) | collective-permute-done | bytes 262176 | tf_op jit(solution)/shard_map/ppermute | solution.py:19
  17.8 3.2 %fusion.469 = (f32[16,64,128]{2,1,0:T(8,128)S(1)}, f32[16,64,128]{2,1,0:T(8,128)}) fusion(f32[1,16,64,128]{3,2,1,0:T(8,128)} %param.21, f32[16,64,128]{2,1,0:T(8,128)S(1)} %copy-done, f32[1,16,64,128]{3,2,1,0:T(8,128)S(1)} %copy-done.10, f32[16,64,128]{2,1,0:T(8,128)S(1)} %bitcast.441, f32[2,16,64,128]{3,2,1,0:T(8,128)S(1)} %constant_dynamic-update-slice_fusion, ...), kind=kLoop, calls=%fused_computation.748 | loop fusion | flops 6553600 | bytes 4718592 | tf_op jit(solution)/shard_map/add | solution.py:92
  22.4 3.2 %fusion.27 = f32[16,64,128]{2,1,0:T(8,128)S(1)} fusion(f32[16,64,128]{2,1,0:T(8,128)S(1)} %bitcast.442, f32[2,16,64,128]{3,2,1,0:T(8,128)} %copy-done.6, f32[2,4,64,128]{3,2,1,0:T(8,128)S(1)} %copy-done.20, f32[2,4,64,128]{3,2,1,0:T(8,128)S(1)} %collective-permute-done, f32[1,16,64,128]{3,2,1,0:T(8,128)S(1)} %copy-done.21, f32[16,64,128]{2,1,0:T(8,128)S(1)} %copy-done), kind=kLoop, calls=%fused_computation.263 | loop fusion | flops 6553600 | bytes 3670016 | tf_op jit(solution)/shard_map/add | solution.py:93
  25.6 2.5 %scatter_fusion = f32[131072]{0:T(1024)S(1)} fusion(f32[131072]{0:T(1024)S(1)} %bitcast.407, s32[256]{0:T(256)S(1)} %bitcast.445, f32[256]{0:T(256)S(1)} %get-tuple-element.105), kind=kCustom, calls=%fused_computation | custom fusion | flops 256 | bytes 4096 | tf_op jit(solution)/shard_map/scatter-add | solution.py:63
  30.1 2.4 %collective-permute-start.3 = (f32[2,4,64,128]{3,2,1,0:T(8,128)S(1)}, f32[2,4,64,128]{3,2,1,0:T(8,128)S(1)}, u32[]{:S(2)}, u32[]{:S(2)}) collective-permute-start(f32[2,4,64,128]{3,2,1,0:T(8,128)S(1)} %get-tuple-element.91), channel_id=1, source_target_pairs={{0,8},{8,16},{16,24},{24,32},{32,40},{40,48},{48,56},{56,64},{64,7... | collective-permute-start | bytes 786440 | tf_op jit(solution)/shard_map/ppermute | solution.py:19
  34.0 5.9 %collective-permute-done.3 = f32[2,4,64,128]{3,2,1,0:T(8,128)S(1)} collective-permute-done((f32[2,4,64,128]{3,2,1,0:T(8,128)S(1)}, f32[2,4,64,128]{3,2,1,0:T(8,128)S(1)}, u32[]{:S(2)}, u32[]{:S(2)}) %collective-permute-start.3) | collective-permute-done | bytes 262176 | tf_op jit(solution)/shard_map/ppermute | solution.py:19
  44.8 2.5 %scatter_fusion.1 = f32[131072]{0:T(1024)S(1)} fusion(f32[131072]{0:T(1024)S(1)} %bitcast.401, s32[256]{0:T(256)S(1)} %bitcast.446, f32[256]{0:T(256)S(1)} %get-tuple-element.104), kind=kCustom, calls=%fused_computation.1 | custom fusion | flops 256 | bytes 4096 | tf_op jit(solution)/shard_map/scatter-add | solution.py:63
  49.3 2.4 %collective-permute-start.5 = (f32[2,4,64,128]{3,2,1,0:T(8,128)S(1)}, f32[2,4,64,128]{3,2,1,0:T(8,128)S(1)}, u32[]{:S(2)}, u32[]{:S(2)}) collective-permute-start(f32[2,4,64,128]{3,2,1,0:T(8,128)S(1)} %get-tuple-element.87), channel_id=1, source_target_pairs={{0,8},{8,16},{16,24},{24,32},{32,40},{40,48},{48,56},{56,64},{64,7... | collective-permute-start | bytes 786440 | tf_op jit(solution)/shard_map/ppermute | solution.py:19
  53.2 5.9 %collective-permute-done.5 = f32[2,4,64,128]{3,2,1,0:T(8,128)S(1)} collective-permute-done((f32[2,4,64,128]{3,2,1,0:T(8,128)S(1)}, f32[2,4,64,128]{3,2,1,0:T(8,128)S(1)}, u32[]{:S(2)}, u32[]{:S(2)}) %collective-permute-start.5) | collective-permute-done | bytes 262176 | tf_op jit(solution)/shard_map/ppermute | solution.py:19
  64.1 2.7 %scatter_fusion.2 = f32[131072]{0:T(1024)S(1)} fusion(f32[131072]{0:T(1024)S(1)} %bitcast.389, s32[256]{0:T(256)S(1)} %bitcast.447, f32[256]{0:T(256)S(1)} %get-tuple-element.103), kind=kCustom, calls=%fused_computation.2 | custom fusion | flops 256 | bytes 4096 | tf_op jit(solution)/shard_map/scatter-add | solution.py:63
  68.8 2.4 %collective-permute-start.7 = (f32[2,4,64,128]{3,2,1,0:T(8,128)S(1)}, f32[2,4,64,128]{3,2,1,0:T(8,128)S(1)}, u32[]{:S(2)}, u32[]{:S(2)}) collective-permute-start(f32[2,4,64,128]{3,2,1,0:T(8,128)S(1)} %get-tuple-element.83), channel_id=1, source_target_pairs={{0,8},{8,16},{16,24},{24,32},{32,40},{40,48},{48,56},{56,64},{64,7... | collective-permute-start | bytes 786440 | tf_op jit(solution)/shard_map/ppermute | solution.py:19
  72.6 5.9 %collective-permute-done.7 = f32[2,4,64,128]{3,2,1,0:T(8,128)S(1)} collective-permute-done((f32[2,4,64,128]{3,2,1,0:T(8,128)S(1)}, f32[2,4,64,128]{3,2,1,0:T(8,128)S(1)}, u32[]{:S(2)}, u32[]{:S(2)}) %collective-permute-start.7) | collective-permute-done | bytes 262176 | tf_op jit(solution)/shard_map/ppermute | solution.py:19
  84.2 2.5 %scatter_fusion.3 = f32[131072]{0:T(1024)S(1)} fusion(f32[131072]{0:T(1024)S(1)} %bitcast.395, s32[256]{0:T(256)S(1)} %bitcast.448, f32[256]{0:T(256)S(1)} %get-tuple-element.102), kind=kCustom, calls=%fused_computation.3 | custom fusion | flops 256 | bytes 4096 | tf_op jit(solution)/shard_map/scatter-add | solution.py:63
  89.7 2.4 %collective-permute-start.9 = (f32[2,4,64,128]{3,2,1,0:T(8,128)S(1)}, f32[2,4,64,128]{3,2,1,0:T(8,128)S(1)}, u32[]{:S(2)}, u32[]{:S(2)}) collective-permute-start(f32[2,4,64,128]{3,2,1,0:T(8,128)S(1)} %get-tuple-element.79), channel_id=1, source_target_pairs={{0,8},{8,16},{16,24},{24,32},{32,40},{40,48},{48,56},{56,64},{64,7... | collective-permute-start | bytes 786440 | tf_op jit(solution)/shard_map/ppermute | solution.py:19
  93.6 5.9 %collective-permute-done.9 = f32[2,4,64,128]{3,2,1,0:T(8,128)S(1)} collective-permute-done((f32[2,4,64,128]{3,2,1,0:T(8,128)S(1)}, f32[2,4,64,128]{3,2,1,0:T(8,128)S(1)}, u32[]{:S(2)}, u32[]{:S(2)}) %collective-permute-start.9) | collective-permute-done | bytes 262176 | tf_op jit(solution)/shard_map/ppermute | solution.py:19
  103.2 2.5 %scatter_fusion.4 = f32[131072]{0:T(1024)S(1)} fusion(f32[131072]{0:T(1024)S(1)} %bitcast.413, s32[256]{0:T(256)S(1)} %bitcast.449, f32[256]{0:T(256)S(1)} %get-tuple-element.101), kind=kCustom, calls=%fused_computation.4 | custom fusion | flops 256 | bytes 4096 | tf_op jit(solution)/shard_map/scatter-add | solution.py:63
  105.7 2.8 %fusion.474 = f32[131072]{0:T(1024)} fusion(f32[131072]{0:T(1024)} %bitcast.437, s32[]{:T(128)} %bitcast.19, f32[1,1]{1,0:T(1,128)} %get-tuple-element.106, s32[1]{0:T(128)S(6)} %copy.24, s32[1]{0:T(128)} %bitcast.18), kind=kLoop, calls=%fused_computation.782 | loop fusion | flops 14 | bytes 2564 | tf_op jit(solution)/shard_map/scatter-add | solution.py:63
  111.6 2.7 %collective-permute-start.11 = (f32[2,4,64,128]{3,2,1,0:T(8,128)S(1)}, f32[2,4,64,128]{3,2,1,0:T(8,128)S(1)}, u32[]{:S(2)}, u32[]{:S(2)}) collective-permute-start(f32[2,4,64,128]{3,2,1,0:T(8,128)S(1)} %get-tuple-element.75), channel_id=1, source_target_pairs={{0,8},{8,16},{16,24},{24,32},{32,40},{40,48},{48,56},{56,64},{64,7... | collective-permute-start | bytes 786440 | tf_op jit(solution)/shard_map/ppermute | solution.py:19
  115.4 6.3 %collective-permute-done.11 = f32[2,4,64,128]{3,2,1,0:T(8,128)S(1)} collective-permute-done((f32[2,4,64,128]{3,2,1,0:T(8,128)S(1)}, f32[2,4,64,128]{3,2,1,0:T(8,128)S(1)}, u32[]{:S(2)}, u32[]{:S(2)}) %collective-permute-start.11) | collective-permute-done | bytes 262176 | tf_op jit(solution)/shard_map/ppermute | solution.py:19
  124.3 6.7 %all-to-all-start = ((f32[8,16,8,128]{3,2,1,0:T(8,128)}), f32[8,16,8,128]{3,2,1,0:T(8,128)S(1)}, u32[]{:S(2)}, u32[]{:S(2)}) async-start(f32[8,16,8,128]{3,2,1,0:T(8,128)} %copy.11), calls=%async_computation | async-start | bytes 1048576 | tf_op jit(solution)/shard_map/all_to_all | solution.py:33
  131.0 3.6 %fusion.200 = f32[16,64,128]{2,1,0:T(8,128)S(1)} fusion(f32[16,64,128]{2,1,0:T(8,128)S(1)} %bitcast.417, f32[2,20,64,128]{3,2,1,0:T(8,128)} %copy-done.2, f32[2,20,64,128]{3,2,1,0:T(8,128)} %copy-done.1, f32[16,64,128]{2,1,0:T(8,128)S(1)} %bitcast.400, f32[16,64,128]{2,1,0:T(8,128)S(1)} %copy-done), kind=kLoop, calls=%fused_computation.436 | loop fusion | flops 5505024 | bytes 6291456 | tf_op jit(solution)/shard_map/add | solution.py:93
  134.5 2.5 %scatter_fusion.5 = f32[131072]{0:T(1024)S(1)} fusion(f32[131072]{0:T(1024)S(1)} %bitcast.443, s32[256]{0:T(256)S(1)} %bitcast.450, f32[256]{0:T(256)S(1)} %get-tuple-element.100), kind=kCustom, calls=%fused_computation.5 | custom fusion | flops 256 | bytes 4096 | tf_op jit(solution)/shard_map/scatter-add | solution.py:63
  137.1 3.7 %all-to-all-done = f32[8,16,8,128]{3,2,1,0:T(8,128)S(1)} async-done(((f32[8,16,8,128]{3,2,1,0:T(8,128)}), f32[8,16,8,128]{3,2,1,0:T(8,128)S(1)}, u32[]{:S(2)}, u32[]{:S(2)}) %all-to-all-start) | async-done | bytes 524320 | tf_op jit(solution)/shard_map/all_to_all | solution.py:33
  (96 shorter events, 48.2 us)
Async XLA Ops:
  1.8 15.9 %copy-start = (f32[16,64,128]{2,1,0:T(8,128)S(1)}, f32[16,64,128]{2,1,0:T(8,128)}, u32[]{:S(2)}) copy-start(f32[16,64,128]{2,1,0:T(8,128)} %param.19) | copy-start | bytes 1572868
  1.8 15.9 %copy-start.10 = (f32[1,16,64,128]{3,2,1,0:T(8,128)S(1)}, f32[1,16,64,128]{3,2,1,0:T(8,128)}, u32[]{:S(2)}) copy-start(f32[1,16,64,128]{3,2,1,0:T(8,128)} %param.20) | copy-start | bytes 1572868
  1.9 19.1 %copy-start.6 = (f32[2,16,64,128]{3,2,1,0:T(8,128)}, f32[2,16,64,128]{3,2,1,0:T(8,128)S(1)}, u32[]{:S(2)}) copy-start(f32[2,16,64,128]{3,2,1,0:T(8,128)S(1)} %constant_dynamic-update-slice_fusion) | copy-start | bytes 3145732
  2.7 8.8 %collective-permute-start = (f32[2,4,64,128]{3,2,1,0:T(8,128)}, f32[2,4,64,128]{3,2,1,0:T(8,128)S(1)}, u32[]{:S(2)}, u32[]{:S(2)}) collective-permute-start(f32[2,4,64,128]{3,2,1,0:T(8,128)} %get-tuple-element.92), channel_id=1, source_target_pairs={{8,0},{16,8},{24,16},{32,24},{40,32},{48,40},{56,48},{64,56},{72,6... | collective-permute-start | bytes 786440 | tf_op jit(solution)/shard_map/ppermute | solution.py:20
  7.3 9.8 %collective-permute-start.1 = (f32[2,4,64,128]{3,2,1,0:T(8,128)S(1)}, f32[2,4,64,128]{3,2,1,0:T(8,128)S(1)}, u32[]{:S(2)}, u32[]{:S(2)}) collective-permute-start(f32[2,4,64,128]{3,2,1,0:T(8,128)S(1)} %get-tuple-element.93), channel_id=1, source_target_pairs={{0,8},{8,16},{16,24},{24,32},{32,40},{40,48},{48,56},{56,64},{64,7... | collective-permute-start | bytes 786440 | tf_op jit(solution)/shard_map/ppermute | solution.py:19
  28.2 5.8 %collective-permute-start.2 = (f32[2,4,64,128]{3,2,1,0:T(8,128)S(1)}, f32[2,4,64,128]{3,2,1,0:T(8,128)S(1)}, u32[]{:S(2)}, u32[]{:S(2)}) collective-permute-start(f32[2,4,64,128]{3,2,1,0:T(8,128)S(1)} %get-tuple-element.90), channel_id=1, source_target_pairs={{8,0},{16,8},{24,16},{32,24},{40,32},{48,40},{56,48},{64,56},{72,6... | collective-permute-start | bytes 786440 | tf_op jit(solution)/shard_map/ppermute | solution.py:20
  30.1 9.8 %collective-permute-start.3 = (f32[2,4,64,128]{3,2,1,0:T(8,128)S(1)}, f32[2,4,64,128]{3,2,1,0:T(8,128)S(1)}, u32[]{:S(2)}, u32[]{:S(2)}) collective-permute-start(f32[2,4,64,128]{3,2,1,0:T(8,128)S(1)} %get-tuple-element.91), channel_id=1, source_target_pairs={{0,8},{8,16},{16,24},{24,32},{32,40},{40,48},{48,56},{56,64},{64,7... | collective-permute-start | bytes 786440 | tf_op jit(solution)/shard_map/ppermute | solution.py:19
  44.8 14.3 %copy-start.3 = (f32[131072]{0:T(1024)}, f32[131072]{0:T(1024)S(1)}, u32[]{:S(2)}) copy-start(f32[131072]{0:T(1024)S(1)} %fusion.471) | copy-start | bytes 1572868
  47.4 5.8 %collective-permute-start.4 = (f32[2,4,64,128]{3,2,1,0:T(8,128)S(1)}, f32[2,4,64,128]{3,2,1,0:T(8,128)S(1)}, u32[]{:S(2)}, u32[]{:S(2)}) collective-permute-start(f32[2,4,64,128]{3,2,1,0:T(8,128)S(1)} %get-tuple-element.86), channel_id=1, source_target_pairs={{8,0},{16,8},{24,16},{32,24},{40,32},{48,40},{56,48},{64,56},{72,6... | collective-permute-start | bytes 786440 | tf_op jit(solution)/shard_map/ppermute | solution.py:20
  49.3 9.8 %collective-permute-start.5 = (f32[2,4,64,128]{3,2,1,0:T(8,128)S(1)}, f32[2,4,64,128]{3,2,1,0:T(8,128)S(1)}, u32[]{:S(2)}, u32[]{:S(2)}) collective-permute-start(f32[2,4,64,128]{3,2,1,0:T(8,128)S(1)} %get-tuple-element.87), channel_id=1, source_target_pairs={{0,8},{8,16},{16,24},{24,32},{32,40},{40,48},{48,56},{56,64},{64,7... | collective-permute-start | bytes 786440 | tf_op jit(solution)/shard_map/ppermute | solution.py:19
  66.8 5.8 %collective-permute-start.6 = (f32[2,4,64,128]{3,2,1,0:T(8,128)S(1)}, f32[2,4,64,128]{3,2,1,0:T(8,128)S(1)}, u32[]{:S(2)}, u32[]{:S(2)}) collective-permute-start(f32[2,4,64,128]{3,2,1,0:T(8,128)S(1)} %get-tuple-element.82), channel_id=1, source_target_pairs={{8,0},{16,8},{24,16},{32,24},{40,32},{48,40},{56,48},{64,56},{72,6... | collective-permute-start | bytes 786440 | tf_op jit(solution)/shard_map/ppermute | solution.py:20
  68.8 9.8 %collective-permute-start.7 = (f32[2,4,64,128]{3,2,1,0:T(8,128)S(1)}, f32[2,4,64,128]{3,2,1,0:T(8,128)S(1)}, u32[]{:S(2)}, u32[]{:S(2)}) collective-permute-start(f32[2,4,64,128]{3,2,1,0:T(8,128)S(1)} %get-tuple-element.83), channel_id=1, source_target_pairs={{0,8},{8,16},{16,24},{24,32},{32,40},{40,48},{48,56},{56,64},{64,7... | collective-permute-start | bytes 786440 | tf_op jit(solution)/shard_map/ppermute | solution.py:19
  86.7 12.8 %copy-start.8 = (f32[131072]{0:T(1024)S(1)}, f32[131072]{0:T(1024)}, u32[]{:S(2)}) copy-start(f32[131072]{0:T(1024)} %copy-done.7) | copy-start | bytes 1572868
  87.8 5.8 %collective-permute-start.8 = (f32[2,4,64,128]{3,2,1,0:T(8,128)S(1)}, f32[2,4,64,128]{3,2,1,0:T(8,128)S(1)}, u32[]{:S(2)}, u32[]{:S(2)}) collective-permute-start(f32[2,4,64,128]{3,2,1,0:T(8,128)S(1)} %get-tuple-element.78), channel_id=1, source_target_pairs={{8,0},{16,8},{24,16},{32,24},{40,32},{48,40},{56,48},{64,56},{72,6... | collective-permute-start | bytes 786440 | tf_op jit(solution)/shard_map/ppermute | solution.py:20
  89.7 9.8 %collective-permute-start.9 = (f32[2,4,64,128]{3,2,1,0:T(8,128)S(1)}, f32[2,4,64,128]{3,2,1,0:T(8,128)S(1)}, u32[]{:S(2)}, u32[]{:S(2)}) collective-permute-start(f32[2,4,64,128]{3,2,1,0:T(8,128)S(1)} %get-tuple-element.79), channel_id=1, source_target_pairs={{0,8},{8,16},{16,24},{24,32},{32,40},{40,48},{48,56},{56,64},{64,7... | collective-permute-start | bytes 786440 | tf_op jit(solution)/shard_map/ppermute | solution.py:19
  108.5 13.1 %copy-start.9 = (f32[131072]{0:T(1024)S(1)}, f32[131072]{0:T(1024)}, u32[]{:S(2)}) copy-start(f32[131072]{0:T(1024)} %fusion.474) | copy-start | bytes 1572868
  109.6 5.8 %collective-permute-start.10 = (f32[2,4,64,128]{3,2,1,0:T(8,128)S(1)}, f32[2,4,64,128]{3,2,1,0:T(8,128)S(1)}, u32[]{:S(2)}, u32[]{:S(2)}) collective-permute-start(f32[2,4,64,128]{3,2,1,0:T(8,128)S(1)} %get-tuple-element.74), channel_id=1, source_target_pairs={{8,0},{16,8},{24,16},{32,24},{40,32},{48,40},{56,48},{64,56},{72,6... | collective-permute-start | bytes 786440 | tf_op jit(solution)/shard_map/ppermute | solution.py:20
  111.5 10.5 %copy-start.12 = (f32[1,16,64,128]{3,2,1,0:T(8,128)S(1)}, f32[1,16,64,128]{3,2,1,0:T(8,128)}, u32[]{:S(2)}) copy-start(f32[1,16,64,128]{3,2,1,0:T(8,128)} %param.22) | copy-start | bytes 1572868
  111.5 10.5 %copy-start.14 = (f32[16,64,128]{2,1,0:T(8,128)S(1)}, f32[16,64,128]{2,1,0:T(8,128)}, u32[]{:S(2)}) copy-start(f32[16,64,128]{2,1,0:T(8,128)} %get-tuple-element.71) | copy-start | bytes 1572868
  111.5 10.5 %copy-start.15 = (f32[16,64,128]{2,1,0:T(8,128)S(1)}, f32[16,64,128]{2,1,0:T(8,128)}, u32[]{:S(2)}) copy-start(f32[16,64,128]{2,1,0:T(8,128)} %get-tuple-element.69) | copy-start | bytes 1572868
  111.5 10.5 %copy-start.16 = (f32[16,64,128]{2,1,0:T(8,128)S(1)}, f32[16,64,128]{2,1,0:T(8,128)}, u32[]{:S(2)}) copy-start(f32[16,64,128]{2,1,0:T(8,128)} %get-tuple-element.67) | copy-start | bytes 1572868
  111.6 10.5 %copy-start.17 = (f32[16,64,128]{2,1,0:T(8,128)S(1)}, f32[16,64,128]{2,1,0:T(8,128)}, u32[]{:S(2)}) copy-start(f32[16,64,128]{2,1,0:T(8,128)} %get-tuple-element.65) | copy-start | bytes 1572868
  111.6 10.1 %collective-permute-start.11 = (f32[2,4,64,128]{3,2,1,0:T(8,128)S(1)}, f32[2,4,64,128]{3,2,1,0:T(8,128)S(1)}, u32[]{:S(2)}, u32[]{:S(2)}) collective-permute-start(f32[2,4,64,128]{3,2,1,0:T(8,128)S(1)} %get-tuple-element.75), channel_id=1, source_target_pairs={{0,8},{8,16},{16,24},{24,32},{32,40},{40,48},{48,56},{56,64},{64,7... | collective-permute-start | bytes 786440 | tf_op jit(solution)/shard_map/ppermute | solution.py:19
  124.3 16.5 %all-to-all-start = ((f32[8,16,8,128]{3,2,1,0:T(8,128)}), f32[8,16,8,128]{3,2,1,0:T(8,128)S(1)}, u32[]{:S(2)}, u32[]{:S(2)}) async-start(f32[8,16,8,128]{3,2,1,0:T(8,128)} %copy.11), calls=%async_computation | async-start | bytes 1048576 | tf_op jit(solution)/shard_map/all_to_all | solution.py:33
  (14 other events, 54.3 us)
where the time goes:
time: 142 us; the launch traced here: 141 us
  other arithmetic  52.3 us (37%)
  waiting for transfers between devices  46.5 us (33%)
  starting transfers between devices  35.1 us (25%)
  local copies, waits for them, and re-layouts  5.17 us (4%)
  between operations  2.37 us (2%)
    ppermute x6, waiting for transfers between devices, extended(): before = lax.ppermute(last, axis, up)  35.6 us
    scatter-add x11, other arithmetic, inject_local(): flat.at[jnp.where(inside, local, 0)].add(jnp.where(inside, values, 0.0))  23.8 us
    ppermute x6, starting transfers between devices, extended(): before = lax.ppermute(last, axis, up)  14.2 us
    ppermute x6, starting transfers between devices, extended(): after = lax.ppermute(leading, axis, down)  14.2 us
    add x6, other arithmetic, body(): 2.0 * qc - qn + speed2 * lq  11.5 us
    add x5, other arithmetic, body(): 2.0 * pc - pn + speed2 * lp  11.2 us
    ppermute x6, waiting for transfers between devices, extended(): after = lax.ppermute(leading, axis, down)  7.27 us
    all_to_all x1, starting transfers between devices, sum_at_owner(): lax.all_to_all(blocks, axis, split_axis=0, concat_axis=0, tiled=True)  6.67 us
  transfers between devices with their start and end apart: 13, of which 13 were waited for; matrix products, arithmetic and copies ran while one was open for 5% of the time, Pallas kernels for 0%

commit v1 on v0

v1 whole, which is shorter than its diff:
```python
import functools
import jax
import jax.numpy as jnp
from jax import lax
from jax.experimental import pallas as pl
from jax.experimental.pallas import tpu as pltpu
from jax.sharding import PartitionSpec as P

STEPS = 6
SCALE = 5040.0
MIDDLE = -14350.0
COEFS = (None, 8064.0, -1008.0, 128.0, -9.0)
PAD = 8
HALO = 8
F32 = jnp.float32

VM = pl.BlockSpec(memory_space=pltpu.VMEM)
SM = pl.BlockSpec(memory_space=pltpu.SMEM)
ANY = pl.BlockSpec(memory_space=pltpu.HBM)


def on_chip(*shape, dtype=F32):
    return pltpu.VMEM(shape, dtype)


def off_chip(value):
    return pltpu.with_memory_space_constraint(value, pltpu.HBM)


def keep(value):
    return pltpu.with_memory_space_constraint(value, pltpu.VMEM)


def params(mib):
    return pltpu.CompilerParams(vmem_limit_bytes=mib << 20)


def cost(us):
    return pl.CostEstimate(flops=int(us * 4e6), bytes_accessed=1 << 20, transcendentals=0)


def pack_kernel(info, pc, pn, qc, qn, speed, near, far, sem):
    rows = speed.shape[0]
    odd = info[1]
    copies = []
    for out, low in ((near, odd), (far, 1 - odd)):
        high = 1 - low
        at = 0
        for src, count in ((pc.at[0], 8), (qc.at[0], 8), (pn.at[0], 4), (qn.at[0], 4), (speed, 4)):
            copies.append(
                pltpu.make_async_copy(
                    src.at[pl.ds(high * (rows - count), count)], out.at[pl.ds(at, count)], sem.at[len(copies)]
                )
            )
            at += count
    for c in copies:
        c.start()
    for c in copies:
        c.wait()


def pack(info, *fields):
    ny, nz = fields[0].shape[2:]
    return pl.pallas_call(
        pack_kernel,
        out_shape=(on_chip(28, ny, nz),) * 2,
        in_specs=[SM] + [ANY] * 5,
        out_specs=(VM,) * 2,
        scratch_shapes=[pltpu.SemaphoreType.DMA((10,))],
        compiler_params=params(4),
        cost_estimate=cost(1.0),
        name="pack",
    )(info, *[off_chip(a) for a in fields])


def load_kernel(info, cells, pc, pn, qc, qn, speed, up, vp, uq, vq, s2, count, order, sem):
    rows, ny = pc.shape[1:3]
    pairs = [
        (src.at[0], dst.at[pl.ds(HALO, rows), pl.ds(PAD, ny)])
        for src, dst in ((pc, up), (pn, vp), (qc, uq), (qn, vq))
    ]
    pairs.append((speed, s2.at[pl.ds(HALO, rows)]))
    copies = [pltpu.make_async_copy(src, dst, sem.at[i]) for i, (src, dst) in enumerate(pairs)]
    for c in copies:
        c.start()
    ext, wide, nz = up.shape
    zero = jnp.zeros((PAD, nz), F32)

    def clear(r, _):
        for ref in (up, vp, uq, vq):
            ref[r, 0:PAD, :] = zero
            ref[r, PAD + ny : wide, :] = zero
        return 0

    lax.fori_loop(0, ext, clear, 0)
    low = (info[0] - 4) * (ny * nz)
    span = (rows + 8) * (ny * nz)

    def find(i, n):
        for j in range(8):
            at = cells[0, i * 8 + j] - low
            order[n] = i * 8 + j
            n = n + jnp.where((at >= 0) & (at < span), 1, 0)
        return n

    count[0] = lax.fori_loop(0, cells.shape[1] // 8, find, 0)
    for c in copies:
        c.wait()

    def square(r, _):
        s2[r] = (s2[r] * s2[r]) * (1.0 / SCALE)
        return 0

    lax.fori_loop(HALO, HALO + rows, square, 0)


def load(info, cells, *fields):
    rows, ny, nz = fields[-1].shape
    ext, wide = rows + 2 * HALO, ny + 2 * PAD
    field = on_chip(ext, wide, nz)
    return pl.pallas_call(
        load_kernel,
        out_shape=(field,) * 4
        + (
            on_chip(ext, ny, nz),
            jax.ShapeDtypeStruct((1,), jnp.int32),
            jax.ShapeDtypeStruct((cells.shape[1] + 8,), jnp.int32),
        ),
        in_specs=[SM, SM] + [ANY] * 5,
        out_specs=(VM,) * 5 + (SM, SM),
        scratch_shapes=[pltpu.SemaphoreType.DMA((5,))],
        compiler_params=params(16),
        cost_estimate=cost(3.0),
        name="load",
    )(info, cells, *[off_chip(f) for f in fields])


GROUP = 2


def fill_weights(weights):
    depth, nz = weights.shape
    gap = lax.broadcasted_iota(jnp.int32, (depth, nz), 0) % nz - lax.broadcasted_iota(jnp.int32, (depth, nz), 1)
    gap = jnp.abs(gap)
    band = jnp.zeros((depth, nz), F32)
    for j in range(1, 5):
        band = jnp.where(gap == j, COEFS[j], band)
    weights[...] = band.astype(jnp.bfloat16)


def along_z(fields, r, weights):
    wide, nz = fields[0].shape[1:]
    ny = wide - 2 * PAD
    parts = []
    for u in fields:
        core = u[pl.ds(r, GROUP), PAD : PAD + ny, :].reshape(GROUP * ny, nz)
        lead = core.astype(jnp.bfloat16)
        rest = (core - lead.astype(F32)).astype(jnp.bfloat16)
        parts.append(jnp.concatenate([lead, rest], axis=1))
    both = jnp.concatenate(parts, axis=0)
    out = jnp.dot(both, weights[...], preferred_element_type=F32)
    return out.reshape(len(fields), GROUP, ny, nz)


def laplace(u, r, z):
    ny = u.shape[1] - 2 * PAD
    core = u[r, PAD : PAD + ny, :]
    total = (3.0 * MIDDLE) * core
    for j in range(1, 5):
        pair = u[r + j, PAD : PAD + ny, :] + u[r - j, PAD : PAD + ny, :]
        pair = pair + (u[r, PAD + j : PAD + j + ny, :] + u[r, PAD - j : PAD - j + ny, :])
        total = total + COEFS[j] * pair
    return core, total + z


def place(u, low, cell, value, start, count):
    ny, nz = u.shape[1] - 2 * PAD, u.shape[2]
    at = cell - low
    r, y, z = at // (ny * nz) + 4, (at // nz) % ny, at % nz
    lane = lax.broadcasted_iota(jnp.int32, (1, nz), 1)
    hit = (lane == z) & (r >= start) & (r < start + count)
    spot = u.at[r, pl.ds(y + PAD, 1), :]
    spot[...] = spot[...] + jnp.where(hit, value, 0.0)


def side_kernel(block, blocks, far, n_in, *refs):
    first_block, last_block = block == 0, block == blocks - 1
    info, wave, source, cells, values, count, order, arrived = refs[:8]
    s2 = refs[12]
    outs = list(refs[n_in:])
    weights = outs.pop()
    sem = outs.pop() if last_block and far else None
    up, vp, uq, vq = (outs.pop(0) for _ in range(4))
    if first_block:
        s2 = outs.pop(0)
    g = outs.pop(0)
    if last_block and far:
        g[...] = refs[13][...]
    ext, ny, nz = up.shape[0], up.shape[1] - 2 * PAD, up.shape[2]
    own = ext - 2 * HALO
    parts = g.shape[0]
    odd = info[1]
    high = odd if far else 1 - odd
    base = (info[0] - 4) * (ny * nz)
    fill_weights(weights)

    edge, edge4 = high * (ext - 8), 4 + high * (ext - 12)

    def eight(i, _):
        up[edge + i, PAD : PAD + ny, :] = arrived[i]
        uq[edge + i, PAD : PAD + ny, :] = arrived[8 + i]
        return 0

    lax.fori_loop(0, 8, eight, 0, unroll=2)
    if first_block:

        def four(i, _):
            vp[edge4 + i, PAD : PAD + ny, :] = arrived[16 + i]
            vq[edge4 + i, PAD : PAD + ny, :] = arrived[20 + i]
            s2[edge4 + i] = (arrived[24 + i] * arrived[24 + i]) * (1.0 / SCALE)
            return 0

        lax.fori_loop(0, 4, four, 0)

    def step(t, pu, pv, qu, qv, begin, rows, mine):
        def trip(i, _):
            r = begin + i * GROUP
            z = along_z((pu, qu), r, weights)
            for j in range(GROUP):
                speed = s2[r + j]
                core, lap = laplace(pu, r + j, z[0, j])
                if pv is not None:
                    pv[r + j, PAD : PAD + ny, :] = 2.0 * core - pv[r + j, PAD : PAD + ny, :] + speed * lap
                core, total = laplace(qu, r + j, z[1, j])
                qv[r + j, PAD : PAD + ny, :] = 2.0 * core - qv[r + j, PAD : PAD + ny, :] + speed * total
                if mine:
                    term = (core * lap).reshape(parts, ny // parts, nz)
                    if not (first_block and t == 0):
                        term = term + g[:, r + j - HALO]
                    g[:, r + j - HALO] = term
            return 0

        lax.fori_loop(0, rows // GROUP, trip, 0)

    def inject(p, q, k, start, rows):
        cell = source[0]
        if p is not None:

            @pl.when((cell >= base) & (cell < base + (own + 8) * (ny * nz)))
            def _():
                place(p, base, cell, wave[0, k], start, rows)

        def one(n, _):
            i = order[n]
            place(q, base, cells[0, i], values[0, k, i], start, rows)
            return 0

        lax.fori_loop(0, count[0], one, 0)

    k = 2 * block
    if far:
        start, rows, mine = 4 + 16 * high, 8, (8 + 12 * high, 4)
    else:
        start, rows, mine = 4 + 8 * high, 16, (8 + 4 * high, 12)
    step(0, up, vp, uq, vq, 4 + 20 * high, 4, False)
    step(0, up, vp, uq, vq, *mine, True)
    inject(vp, vq, k, start, rows)
    half = 8 + 8 * high
    step(1, vp, None if last_block else up, vq, uq, half, 8, True)
    inject(None if last_block else up, uq, k + 1, half, 8)
    if not last_block:
        (send,) = outs

        def out(i, _):
            send[i] = up[half + i, PAD : PAD + ny, :]
            send[8 + i] = uq[half + i, PAD : PAD + ny, :]
            return 0

        lax.fori_loop(0, 8, out, 0, unroll=2)
    elif far:
        (final,) = outs
        done = pltpu.make_async_copy(uq.at[pl.ds(HALO, own), pl.ds(PAD, ny)], final.at[0], sem)
        done.start()
        done.wait()


def side(block, blocks, far, parts, scalars, arrived, fields, s2, g):
    first_block, last_block = block == 0, block == blocks - 1
    ext, ny, nz = s2.shape
    own = ext - 2 * HALO
    end = last_block and far
    args = [*scalars, keep(arrived), *[keep(f) for f in fields], keep(s2)]
    field = on_chip(*fields[0].shape)
    outs, alias = [field] * 4, {8: 0, 9: 1, 10: 2, 11: 3}
    if first_block:
        alias[12] = 4
        outs.append(on_chip(*s2.shape))
    if g is not None:
        args.append(keep(g))
        if not end:
            alias[13] = len(outs)
    outs.append(jax.ShapeDtypeStruct((parts, own, ny // parts, nz), F32) if end else on_chip(parts, own, ny // parts, nz))
    specs = [VM] * len(outs)
    scratch = [pltpu.VMEM((2 * nz, nz), jnp.bfloat16)]
    if not last_block:
        outs.append(on_chip(16, ny, nz))
        specs.append(VM)
    elif far:
        outs.append(jax.ShapeDtypeStruct((1, own, ny, nz), F32))
        specs.append(ANY)
        scratch.insert(0, pltpu.SemaphoreType.DMA)
    res = list(
        pl.pallas_call(
            functools.partial(side_kernel, block, blocks, far, len(args)),
            out_shape=tuple(outs),
            in_specs=[SM] * 7 + [VM] * (len(args) - 7),
            out_specs=tuple(specs),
            scratch_shapes=scratch,
            input_output_aliases=alias,
            compiler_params=params(16),
            cost_estimate=cost(4.0),
            name=("far" if far else "near") + f"{block}",
        )(*args)
    )
    fields = res[:4]
    if first_block:
        s2 = res.pop(4)
    return fields, s2, res[4], res[5] if len(res) > 5 else None


def swap_near(value, axis):
    return lax.ppermute(value, axis, [(i, i ^ 1) for i in range(lax.axis_size(axis))])


def swap_far(value, axis):
    count = lax.axis_size(axis)
    return lax.ppermute(value, axis, [(i, i + 1 if i % 2 else i - 1) for i in range(1, count - 1)])


def body(courant, p_current, p_later, q_current, q_later, wavelet, source_cell, receiver_cells, residual_data):
    rows = courant.shape[0]
    shots = lax.axis_size("shot")
    blocks = STEPS // 2
    index = lax.axis_index("space").astype(jnp.int32)
    info = jnp.stack([index * rows, index % 2])
    near, far = pack(info, p_current, p_later, q_current, q_later, courant)
    near = swap_near(near, "space")
    far = swap_far(far, "space")
    *fields, s2, count, order = load(info, receiver_cells, p_current, p_later, q_current, q_later, courant)
    scalars = (info, wavelet, source_cell, receiver_cells, residual_data, count, order)
    g = None
    for b in range(blocks):
        last = b == blocks - 1
        fields, s2, g, out = side(b, blocks, False, shots, scalars, near, fields, s2, g)
        if not last:
            near = swap_near(out, "space")
        fields, s2, g, out = side(b, blocks, True, shots, scalars, far, fields, s2, g)
        if not last:
            far = swap_far(out, "space")
    arrived = lax.all_to_all(g, "shot", split_axis=0, concat_axis=0, tiled=True)
    gradient = arrived.sum(axis=0) * (1.0 / (SCALE * STEPS * shots))
    return gradient, out


def solution(mesh):
    in_specs = (
        P("space", None, None),
        P("shot", "space", None, None),
        P("shot", "space", None, None),
        P("shot", "space", None, None),
        P("shot", "space", None, None),
        P("shot", None),
        P("shot"),
        P("shot", None),
        P("shot", None, None),
    )
    out_specs = (P("space", "shot", None), P("shot", "space", None, None))
    return jax.shard_map(body, mesh=mesh, in_specs=in_specs, out_specs=out_specs, check_vma=False)
```

time: 142 us -> 90.1 us (0.63)
  the two profiles are of different devices: /device:TPU:384 before, /device:TPU:322 now
where the time goes in v1:
time: 90.1 us; the launch traced here: 89.5 us
  Pallas kernels  31.8 us (35%)
  waiting for transfers between devices  21 us (23%)
  blocking collectives  20.7 us (23%)
  starting transfers between devices  13.8 us (15%)
  between operations  1.46 us (2%)
    pallas_call x6, Pallas kernels, side(): pl.pallas_call(functools.partial(side_kernel, block, blocks, far, len(arg...  26.8 us
    ppermute x3, waiting for transfers between devices, swap_far(): lax.ppermute(value, axis, [(i, i + 1 if i % 2 else i - 1) for i in range(...  21 us
    all_to_all x1, blocking collectives, body(): arrived = lax.all_to_all(g, 'shot', split_axis=0, concat_axis=0, tiled=True)  20.7 us
    ppermute x3, starting transfers between devices, swap_far(): lax.ppermute(value, axis, [(i, i + 1 if i % 2 else i - 1) for i in range(...  7.64 us
    ppermute x3, starting transfers between devices, swap_near(): lax.ppermute(value, axis, [(i, i ^ 1) for i in range(lax.axis_size(axis))])  6.17 us
    pallas_call x1, Pallas kernels, load(): pl.pallas_call(load_kernel, out_shape=(field,) * 4 + (on_chip(ext, ny, nz...  2.98 us
    pallas_call x1, Pallas kernels, pack(): pl.pallas_call(pack_kernel, out_shape=(on_chip(28, ny, nz),) * 2, in_spec...  2.05 us
  transfers between devices with their start and end apart: 6, of which 3 were waited for; matrix products, arithmetic and copies ran while one was open for 0% of the time, Pallas kernels for 28%

profile of v1, /device:TPU:322, one launch (start us, length us, event | category | flops | bytes accessed | tf_op | source)
XLA Modules:
  0.0 89.5 jit_solution(14588807720157292978)
XLA Ops:
  0.6 0.1 pad_add_fusion.info.refs_0_
  0.7 2.0 %pack.1 = (f32[28,64,128]{2,1,0:T(8,128)S(1)}, f32[28,64,128]{2,1,0:T(8,128)S(1)}) custom-call(s32[2]{0:T(128)S(1)} %pad_add_fusion.info.refs_0_, f32[1,16,64,128]{3,2,1,0:T(8,128)} %pc.3, f32[1,16,64,128]{3,2,1,0:T(8,128)} %pn.3, f32[1,16,64,128]{3,2,1,0:T(8,128)} %qc.3, f32[1,16,64,128]{3,2,1,0:T(8,128)} %qn.3, f32[16,64,128]{2,1,0:T(8,128)} %speed.3), custom_call_target="tpu_custom_call" | custom-call | flops 4000000 | bytes 1048576 | tf_op jit(solution)/shard_map/pack/pallas_call | solution.py:64
  2.8 1.9 %collective-permute-start.1 = (f32[28,64,128]{2,1,0:T(8,128)S(1)}, f32[28,64,128]{2,1,0:T(8,128)S(1)}, u32[]{:S(2)}, u32[]{:S(2)}) collective-permute-start(f32[28,64,128]{2,1,0:T(8,128)S(1)} %get-tuple-element.47), channel_id=1, source_target_pairs={{0,8},{8,0},{16,24},{24,16},{32,40},{40,32},{48,56},{56,48},{64,72... | collective-permute-start | bytes 2752520 | tf_op jit(solution)/shard_map/ppermute | solution.py:332
  4.7 2.5 %collective-permute-start = (f32[28,64,128]{2,1,0:T(8,128)S(1)}, f32[28,64,128]{2,1,0:T(8,128)S(1)}, u32[]{:S(2)}, u32[]{:S(2)}) collective-permute-start(f32[28,64,128]{2,1,0:T(8,128)S(1)} %get-tuple-element.46), channel_id=1, source_target_pairs={{8,16},{16,8},{24,32},{32,24},{40,48},{48,40},{56,64},{64,56},{72,... | collective-permute-start | bytes 2752520 | tf_op jit(solution)/shard_map/ppermute | solution.py:337
  7.9 0.0 copy-start.1
  7.9 3.0 %load.1 = (f32[32,80,128]{2,1,0:T(8,128)S(1)}, f32[32,80,128]{2,1,0:T(8,128)S(1)}, f32[32,80,128]{2,1,0:T(8,128)S(1)}, f32[32,80,128]{2,1,0:T(8,128)S(1)}, f32[3...) custom-call(s32[2]{0:T(128)S(1)} %pad_add_fusion.info.refs_0_, s32[1,256]{1,0:T(1,128)S(1)} %copy-done, ...), custom_call_target="tpu_custom_call" | custom-call | flops 12000000 | bytes 1048576 | tf_op jit(solution)/shard_map/load/pallas_call | solution.py:121
  10.9 0.0 collective-permute-done.1.refs_7_
  11.0 4.9 %near0.1 = (f32[32,80,128]{2,1,0:T(8,128)S(1)}, f32[32,80,128]{2,1,0:T(8,128)S(1)}, f32[32,80,128]{2,1,0:T(8,128)S(1)}, f32[32,80,128]{2,1,0:T(8,128)S(1)}, f32[...) custom-call(s32[2]{0:T(128)S(1)} %pad_add_fusion.info.refs_0_, ...), custom_call_target="tpu_custom_call", output_to_operand_aliasing={{0}: (8, {}), {1}: (9, {}), {2}: (10, {}), {3}: (11, {}), {... | custom-call | flops 16000000 | bytes 1048576 | tf_op jit(solution)/shard_map/near0/pallas_call | solution.py:313
  15.8 2.3 %collective-permute-start.3 = (f32[16,64,128]{2,1,0:T(8,128)S(1)}, f32[16,64,128]{2,1,0:T(8,128)S(1)}, u32[]{:S(2)}, u32[]{:S(2)}) collective-permute-start(f32[16,64,128]{2,1,0:T(8,128)S(1)} %get-tuple-element.60), channel_id=1, source_target_pairs={{0,8},{8,0},{16,24},{24,16},{32,40},{40,32},{48,56},{56,48},{64,72... | collective-permute-start | bytes 1572872 | tf_op jit(solution)/shard_map/ppermute | solution.py:332
  18.2 11.1 %collective-permute-done.refs_7_ = f32[28,64,128]{2,1,0:T(8,128)S(1)} collective-permute-done((f32[28,64,128]{2,1,0:T(8,128)S(1)}, f32[28,64,128]{2,1,0:T(8,128)S(1)}, u32[]{:S(2)}, u32[]{:S(2)}) %collective-permute-start) | collective-permute-done | bytes 917536 | tf_op jit(solution)/shard_map/ppermute | solution.py:337
  29.2 3.9 %far0.1 = (f32[32,80,128]{2,1,0:T(8,128)S(1)}, f32[32,80,128]{2,1,0:T(8,128)S(1)}, f32[32,80,128]{2,1,0:T(8,128)S(1)}, f32[32,80,128]{2,1,0:T(8,128)S(1)}, f32[3...) custom-call(s32[2]{0:T(128)S(1)} %pad_add_fusion.info.refs_0_, ...), custom_call_target="tpu_custom_call", output_to_operand_aliasing={{0}: (8, {}), {1}: (9, {}), {2}: (10, {}), {3}: (11, {}), {... | custom-call | flops 16000000 | bytes 1048576 | tf_op jit(solution)/shard_map/far0/pallas_call | solution.py:313
  33.1 2.5 %collective-permute-start.2 = (f32[16,64,128]{2,1,0:T(8,128)S(1)}, f32[16,64,128]{2,1,0:T(8,128)S(1)}, u32[]{:S(2)}, u32[]{:S(2)}) collective-permute-start(f32[16,64,128]{2,1,0:T(8,128)S(1)} %get-tuple-element.59), channel_id=1, source_target_pairs={{8,16},{16,8},{24,32},{32,24},{40,48},{48,40},{56,64},{64,56},{72,... | collective-permute-start | bytes 1572872 | tf_op jit(solution)/shard_map/ppermute | solution.py:337
  35.7 0.0 collective-permute-done.3.refs_7_
  35.7 4.9 %near1.1 = (f32[32,80,128]{2,1,0:T(8,128)S(1)}, f32[32,80,128]{2,1,0:T(8,128)S(1)}, f32[32,80,128]{2,1,0:T(8,128)S(1)}, f32[32,80,128]{2,1,0:T(8,128)S(1)}, f32[...) custom-call(s32[2]{0:T(128)S(1)} %pad_add_fusion.info.refs_0_, ...), custom_call_target="tpu_custom_call", output_to_operand_aliasing={{0}: (8, {}), {1}: (9, {}), {2}: (10, {}), {3}: (11, {}), {... | custom-call | flops 16000000 | bytes 1048576 | tf_op jit(solution)/shard_map/near1/pallas_call | solution.py:313
  40.6 1.9 %collective-permute-start.5 = (f32[16,64,128]{2,1,0:T(8,128)S(1)}, f32[16,64,128]{2,1,0:T(8,128)S(1)}, u32[]{:S(2)}, u32[]{:S(2)}) collective-permute-start(f32[16,64,128]{2,1,0:T(8,128)S(1)} %get-tuple-element.73), channel_id=1, source_target_pairs={{0,8},{8,0},{16,24},{24,16},{32,40},{40,32},{48,56},{56,48},{64,72... | collective-permute-start | bytes 1572872 | tf_op jit(solution)/shard_map/ppermute | solution.py:332
  42.5 1.1 %collective-permute-done.2.refs_7_ = f32[16,64,128]{2,1,0:T(8,128)S(1)} collective-permute-done((f32[16,64,128]{2,1,0:T(8,128)S(1)}, f32[16,64,128]{2,1,0:T(8,128)S(1)}, u32[]{:S(2)}, u32[]{:S(2)}) %collective-permute-start.2) | collective-permute-done | bytes 524320 | tf_op jit(solution)/shard_map/ppermute | solution.py:337
  43.6 3.9 %far1.1 = (f32[32,80,128]{2,1,0:T(8,128)S(1)}, f32[32,80,128]{2,1,0:T(8,128)S(1)}, f32[32,80,128]{2,1,0:T(8,128)S(1)}, f32[32,80,128]{2,1,0:T(8,128)S(1)}, f32[8...) custom-call(s32[2]{0:T(128)S(1)} %pad_add_fusion.info.refs_0_, ...), custom_call_target="tpu_custom_call", output_to_operand_aliasing={{0}: (8, {}), {1}: (9, {}), {2}: (10, {}), {3}: (11, {}), {... | custom-call | flops 16000000 | bytes 1048576 | tf_op jit(solution)/shard_map/far1/pallas_call | solution.py:313
  47.5 2.5 %collective-permute-start.4 = (f32[16,64,128]{2,1,0:T(8,128)S(1)}, f32[16,64,128]{2,1,0:T(8,128)S(1)}, u32[]{:S(2)}, u32[]{:S(2)}) collective-permute-start(f32[16,64,128]{2,1,0:T(8,128)S(1)} %get-tuple-element.72), channel_id=1, source_target_pairs={{8,16},{16,8},{24,32},{32,24},{40,48},{48,40},{56,64},{64,56},{72,... | collective-permute-start | bytes 1572872 | tf_op jit(solution)/shard_map/ppermute | solution.py:337
  50.0 0.0 collective-permute-done.5.refs_7_
  50.1 4.7 %near2.1 = (f32[32,80,128]{2,1,0:T(8,128)S(1)}, f32[32,80,128]{2,1,0:T(8,128)S(1)}, f32[32,80,128]{2,1,0:T(8,128)S(1)}, f32[32,80,128]{2,1,0:T(8,128)S(1)}, f32[8,16,8,128]{3,2,1,0:T(8,128)S(1)}) custom-call(s32[2]{0:T(128)S(1)} %pad_add_fusion.info.refs_0_, ...), custom_call_target="tpu_custom_call", output_to_operand_aliasing={{0}: (8, {}), {1}: (9, {}), {2}: (10, {}), {3}: (11, {}), {... | custom-call | flops 16000000 | bytes 1048576 | tf_op jit(solution)/shard_map/near2/pallas_call | solution.py:313
  54.8 8.8 %collective-permute-done.4.refs_7_ = f32[16,64,128]{2,1,0:T(8,128)S(1)} collective-permute-done((f32[16,64,128]{2,1,0:T(8,128)S(1)}, f32[16,64,128]{2,1,0:T(8,128)S(1)}, u32[]{:S(2)}, u32[]{:S(2)}) %collective-permute-start.4) | collective-permute-done | bytes 524320 | tf_op jit(solution)/shard_map/ppermute | solution.py:337
  63.6 4.6 %far2.1 = (f32[32,80,128]{2,1,0:T(8,128)S(1)}, f32[32,80,128]{2,1,0:T(8,128)S(1)}, f32[32,80,128]{2,1,0:T(8,128)S(1)}, f32[32,80,128]{2,1,0:T(8,128)S(1)}, f32[8...) custom-call(s32[2]{0:T(128)S(1)} %pad_add_fusion.info.refs_0_, ...), custom_call_target="tpu_custom_call", output_to_operand_aliasing={{0}: (8, {}), {1}: (9, {}), {2}: (10, {}), {3}: (11, {})} | custom-call | flops 16000000 | bytes 1048576 | tf_op jit(solution)/shard_map/far2/pallas_call | solution.py:313
  68.2 20.7 %all_to_all.5 = f32[8,16,8,128]{3,2,1,0:T(8,128)S(1)} all-to-all(f32[8,16,8,128]{3,2,1,0:T(8,128)S(1)} %get-tuple-element.84), channel_id=1, replica_groups=mesh['space'=64,'shot'=8] {'shot'}, dimensions={0} | all-to-all | bytes 1048576 | tf_op jit(solution)/shard_map/all_to_all | solution.py:360
  88.9 0.6 broadcast_multiply_fusion
  (7 shorter events, 0.0 us)
Async XLA Ops:
  0.7 7.2 %copy-start.2 = (f32[1,6,256]{2,0,1:T(1,128)S(1)}, f32[1,6,256]{2,0,1:T(1,128)}, u32[]{:S(2)}) copy-start(f32[1,6,256]{2,0,1:T(1,128)} %param.17) | copy-start | bytes 18436
  0.7 7.2 %copy-start = (s32[1,256]{1,0:T(1,128)S(1)}, s32[1,256]{1,0:T(1,128)}, u32[]{:S(2)}) copy-start(s32[1,256]{1,0:T(1,128)} %refs_3_.11) | copy-start | bytes 3076
  2.8 8.2 %collective-permute-start.1 = (f32[28,64,128]{2,1,0:T(8,128)S(1)}, f32[28,64,128]{2,1,0:T(8,128)S(1)}, u32[]{:S(2)}, u32[]{:S(2)}) collective-permute-start(f32[28,64,128]{2,1,0:T(8,128)S(1)} %get-tuple-element.47), channel_id=1, source_target_pairs={{0,8},{8,0},{16,24},{24,16},{32,40},{40,32},{48,56},{56,48},{64,72... | collective-permute-start | bytes 2752520 | tf_op jit(solution)/shard_map/ppermute | solution.py:332
  4.7 24.5 %collective-permute-start = (f32[28,64,128]{2,1,0:T(8,128)S(1)}, f32[28,64,128]{2,1,0:T(8,128)S(1)}, u32[]{:S(2)}, u32[]{:S(2)}) collective-permute-start(f32[28,64,128]{2,1,0:T(8,128)S(1)} %get-tuple-element.46), channel_id=1, source_target_pairs={{8,16},{16,8},{24,32},{32,24},{40,48},{48,40},{56,64},{64,56},{72,... | collective-permute-start | bytes 2752520 | tf_op jit(solution)/shard_map/ppermute | solution.py:337
  7.9 3.0 %copy-start.1 = (f32[1,6]{1,0:T(1,128)S(1)}, f32[1,6]{1,0:T(1,128)}, u32[]{:S(2)}) copy-start(f32[1,6]{1,0:T(1,128)} %refs_1_.11) | copy-start | bytes 76
  15.8 19.9 %collective-permute-start.3 = (f32[16,64,128]{2,1,0:T(8,128)S(1)}, f32[16,64,128]{2,1,0:T(8,128)S(1)}, u32[]{:S(2)}, u32[]{:S(2)}) collective-permute-start(f32[16,64,128]{2,1,0:T(8,128)S(1)} %get-tuple-element.60), channel_id=1, source_target_pairs={{0,8},{8,0},{16,24},{24,16},{32,40},{40,32},{48,56},{56,48},{64,72... | collective-permute-start | bytes 1572872 | tf_op jit(solution)/shard_map/ppermute | solution.py:332
  33.1 10.5 %collective-permute-start.2 = (f32[16,64,128]{2,1,0:T(8,128)S(1)}, f32[16,64,128]{2,1,0:T(8,128)S(1)}, u32[]{:S(2)}, u32[]{:S(2)}) collective-permute-start(f32[16,64,128]{2,1,0:T(8,128)S(1)} %get-tuple-element.59), channel_id=1, source_target_pairs={{8,16},{16,8},{24,32},{32,24},{40,48},{48,40},{56,64},{64,56},{72,... | collective-permute-start | bytes 1572872 | tf_op jit(solution)/shard_map/ppermute | solution.py:337
  40.6 9.5 %collective-permute-start.5 = (f32[16,64,128]{2,1,0:T(8,128)S(1)}, f32[16,64,128]{2,1,0:T(8,128)S(1)}, u32[]{:S(2)}, u32[]{:S(2)}) collective-permute-start(f32[16,64,128]{2,1,0:T(8,128)S(1)} %get-tuple-element.73), channel_id=1, source_target_pairs={{0,8},{8,0},{16,24},{24,16},{32,40},{40,32},{48,56},{56,48},{64,72... | collective-permute-start | bytes 1572872 | tf_op jit(solution)/shard_map/ppermute | solution.py:332
  47.5 16.1 %collective-permute-start.4 = (f32[16,64,128]{2,1,0:T(8,128)S(1)}, f32[16,64,128]{2,1,0:T(8,128)S(1)}, u32[]{:S(2)}, u32[]{:S(2)}) collective-permute-start(f32[16,64,128]{2,1,0:T(8,128)S(1)} %get-tuple-element.72), channel_id=1, source_target_pairs={{8,16},{16,8},{24,32},{32,24},{40,48},{48,40},{56,64},{64,56},{72,... | collective-permute-start | bytes 1572872 | tf_op jit(solution)/shard_map/ppermute | solution.py:337

commit v2 on v1

v2 whole, which is shorter than its diff:
```python
import functools
import jax
import jax.numpy as jnp
from jax import lax
from jax.experimental import pallas as pl
from jax.experimental.pallas import tpu as pltpu
from jax.sharding import PartitionSpec as P

STEPS = 6
SCALE = 5040.0
MIDDLE = -14350.0
COEFS = (None, 8064.0, -1008.0, 128.0, -9.0)
PAD = 8
HALO = 8
F32 = jnp.float32

VM = pl.BlockSpec(memory_space=pltpu.VMEM)
SM = pl.BlockSpec(memory_space=pltpu.SMEM)
ANY = pl.BlockSpec(memory_space=pltpu.HBM)


def on_chip(*shape, dtype=F32):
    return pltpu.VMEM(shape, dtype)


def off_chip(value):
    return pltpu.with_memory_space_constraint(value, pltpu.HBM)


def keep(value):
    return pltpu.with_memory_space_constraint(value, pltpu.VMEM)


def params(mib):
    return pltpu.CompilerParams(vmem_limit_bytes=mib << 20)


def cost(us):
    return pl.CostEstimate(flops=int(us * 4e6), bytes_accessed=1 << 20, transcendentals=0)


def rows_out(high, rows, out, parts, sem, base):
    copies, at = [], 0
    for src, count in parts:
        copies.append(
            pltpu.make_async_copy(
                src.at[pl.ds(high * (rows - count), count)], out.at[pl.ds(at, count)], sem.at[base + len(copies)]
            )
        )
        at += count
    return copies


def pack_kernel(info, pc, pn, qc, qn, speed, near, far, sem):
    rows = speed.shape[0]
    odd = info[1]
    p, q, p_old, q_old = (ref.at[0] for ref in (pc, qc, pn, qn))
    copies = rows_out(1 - odd, rows, near, ((p, 8), (q, 8), (p_old, 4), (q_old, 4), (speed, 4)), sem, 0)
    copies += rows_out(odd, rows, far, ((p, 8), (p_old, 4), (speed, 4)), sem, 5)
    for c in copies:
        c.start()
    for c in copies:
        c.wait()


def pack(info, *fields):
    ny, nz = fields[0].shape[2:]
    return pl.pallas_call(
        pack_kernel,
        out_shape=(on_chip(28, ny, nz), on_chip(16, ny, nz)),
        in_specs=[SM] + [ANY] * 5,
        out_specs=(VM,) * 2,
        scratch_shapes=[pltpu.SemaphoreType.DMA((8,))],
        compiler_params=params(4),
        cost_estimate=cost(1.0),
        name="pack",
    )(info, *[off_chip(a) for a in fields])


def load_kernel(info, cells, values, pc, pn, qc, qn, speed, up, vp, uq, vq, s2, added, weights, far, order, sem):
    rows, ny = pc.shape[1:3]
    pairs = [
        (src.at[0], dst.at[pl.ds(HALO, rows), pl.ds(PAD, ny)])
        for src, dst in ((pc, up), (pn, vp), (qc, uq), (qn, vq))
    ]
    pairs.append((speed, s2.at[pl.ds(HALO, rows)]))
    copies = [pltpu.make_async_copy(src, dst, sem.at[i]) for i, (src, dst) in enumerate(pairs)]
    copies += rows_out(info[1], rows, far, ((qc.at[0], 8), (qn.at[0], 4)), sem, 5)
    for c in copies:
        c.start()
    ext, wide, nz = up.shape
    zero = jnp.zeros((PAD, nz), F32)

    def clear(r, _):
        for ref in (up, vp, uq, vq):
            ref[r, 0:PAD, :] = zero
            ref[r, PAD + ny : wide, :] = zero
        return 0

    lax.fori_loop(0, ext, clear, 0)
    fill_weights(weights)
    steps, near_rows = added.shape[:2]
    blank = jnp.zeros((ny, nz), F32)

    def clear_added(r, _):
        for k in range(steps):
            added[k, r] = blank
        return 0

    lax.fori_loop(0, near_rows, clear_added, 0)
    low = (info[0] - 4) * (ny * nz)
    span = (rows + 8) * (ny * nz)

    def find(i, n):
        for j in range(8):
            at = cells[0, i * 8 + j] - low
            order[n] = i * 8 + j
            n = n + jnp.where((at >= 0) & (at < span), 1, 0)
        return n

    count = lax.fori_loop(0, cells.shape[1] // 8, find, 0)
    lane = lax.broadcasted_iota(jnp.int32, (1, nz), 1)

    def collect(n, _):
        i = order[n]
        at = cells[0, i] - low
        r, y, z = at // (ny * nz), (at // nz) % ny, at % nz
        spots = [added.at[k, r, pl.ds(y, 1), :] for k in range(steps)]
        new = [spot[...] + jnp.where(lane == z, values[0, k, i], 0.0) for k, spot in enumerate(spots)]
        for spot, value in zip(spots, new):
            spot[...] = value
        return 0

    lax.fori_loop(0, count, collect, 0)
    for c in copies:
        c.wait()

    def square(r, _):
        s2[r] = (s2[r] * s2[r]) * (1.0 / SCALE)
        return 0

    lax.fori_loop(HALO, HALO + rows, square, 0)


def load(info, cells, values, *fields):
    rows, ny, nz = fields[-1].shape
    ext, wide = rows + 2 * HALO, ny + 2 * PAD
    field = on_chip(ext, wide, nz)
    return pl.pallas_call(
        load_kernel,
        out_shape=(field,) * 4
        + (
            on_chip(ext, ny, nz),
            on_chip(values.shape[1], rows + 8, ny, nz),
            on_chip(2 * nz, nz, dtype=jnp.bfloat16),
            on_chip(12, ny, nz),
        ),
        in_specs=[SM] * 3 + [ANY] * 5,
        out_specs=(VM,) * 8,
        scratch_shapes=[pltpu.SMEM((cells.shape[1] + 8,), jnp.int32), pltpu.SemaphoreType.DMA((7,))],
        compiler_params=params(16),
        cost_estimate=cost(3.0),
        name="load",
    )(info, cells, values, *[off_chip(f) for f in fields])


GROUP = 4


def fill_weights(weights):
    depth, nz = weights.shape
    gap = lax.broadcasted_iota(jnp.int32, (depth, nz), 0) % nz - lax.broadcasted_iota(jnp.int32, (depth, nz), 1)
    gap = jnp.abs(gap)
    band = jnp.zeros((depth, nz), F32)
    for j in range(1, 5):
        band = jnp.where(gap == j, COEFS[j], band)
    weights[...] = band.astype(jnp.bfloat16)


def along_z(fields, r, weights):
    wide, nz = fields[0].shape[1:]
    ny = wide - 2 * PAD
    parts = []
    for u in fields:
        core = u[pl.ds(r, GROUP), PAD : PAD + ny, :].reshape(GROUP * ny, nz)
        lead = core.astype(jnp.bfloat16)
        rest = (core - lead.astype(F32)).astype(jnp.bfloat16)
        parts.append(jnp.concatenate([lead, rest], axis=1))
    both = jnp.concatenate(parts, axis=0)
    out = jnp.dot(both, weights[...], preferred_element_type=F32)
    return out.reshape(len(fields), GROUP, ny, nz)


def laplace(u, r, z):
    ny = u.shape[1] - 2 * PAD
    core = u[r, PAD : PAD + ny, :]
    total = (3.0 * MIDDLE) * core
    for j in range(1, 5):
        pair = u[r + j, PAD : PAD + ny, :] + u[r - j, PAD : PAD + ny, :]
        pair = pair + (u[r, PAD + j : PAD + j + ny, :] + u[r, PAD - j : PAD - j + ny, :])
        total = total + COEFS[j] * pair
    return core, total + z


def place(u, low, cell, value, start, count):
    ny, nz = u.shape[1] - 2 * PAD, u.shape[2]
    at = cell - low
    r, y, z = at // (ny * nz) + 4, (at // nz) % ny, at % nz
    lane = lax.broadcasted_iota(jnp.int32, (1, nz), 1)
    hit = (lane == z) & (r >= start) & (r < start + count)
    spot = u.at[r, pl.ds(y + PAD, 1), :]
    spot[...] = spot[...] + jnp.where(hit, value, 0.0)


def field_step(u, v, begin, rows, s2, weights, after):
    ny = u[0].shape[1] - 2 * PAD

    def trip(i, _):
        r = begin + i * GROUP
        z = along_z(u, r, weights)
        for j in range(GROUP):
            speed = s2[r + j]
            seen = []
            for n, (now, new) in enumerate(zip(u, v)):
                core, total = laplace(now, r + j, z[n, j])
                more = after(n, r + j, core, total, seen)
                seen.append(total)
                if new is not None:
                    value = 2.0 * core - new[r + j, PAD : PAD + ny, :] + speed * total
                    new[r + j, PAD : PAD + ny, :] = value if more is None else value + more
        return 0

    lax.fori_loop(0, rows // GROUP, trip, 0)


def add_image(g, r, product, fresh):
    parts, _, rest, nz = g.shape
    term = product.reshape(parts, rest, nz)
    g[:, r - HALO] = term if fresh else term + g[:, r - HALO]


def add_source(info, source, wave, k, p, start, rows):
    ext, ny, nz = p.shape[0], p.shape[1] - 2 * PAD, p.shape[2]
    base = (info[0] - 4) * (ny * nz)
    cell = source[0]

    @pl.when((cell >= base) & (cell < base + (ext - 8) * (ny * nz)))
    def _():
        place(p, base, cell, wave[0, k], start, rows)


def rows_in(dst, at, src, start, count):
    ny = src.shape[1]

    def one(i, _):
        dst[at + i, PAD : PAD + ny, :] = src[start + i]
        return 0

    lax.fori_loop(0, count, one, 0, unroll=2)


def speed_in(s2, at, src, start):
    def one(i, _):
        s2[at + i] = (src[start + i] * src[start + i]) * (1.0 / SCALE)
        return 0

    lax.fori_loop(0, 4, one, 0)


def rows_back(send, at, u, start):
    ny = send.shape[1]

    def one(i, _):
        send[at + i] = u[start + i, PAD : PAD + ny, :]
        return 0

    lax.fori_loop(0, 8, one, 0, unroll=2)


def near_kernel(block, blocks, n_in, *refs):
    first_block, last_block = block == 0, block == blocks - 1
    info, wave, source, added, weights, arrived = refs[:6]
    s2 = refs[10]
    outs = list(refs[n_in:])
    up, vp, uq, vq = (outs.pop(0) for _ in range(4))
    if first_block:
        s2 = outs.pop(0)
    g = outs.pop(0)
    ext = up.shape[0]
    high = 1 - info[1]
    edge, edge4 = high * (ext - 8), 4 + high * (ext - 12)
    rows_in(up, edge, arrived, 0, 8)
    rows_in(uq, edge, arrived, 8, 8)
    if first_block:
        rows_in(vp, edge4, arrived, 16, 4)
        rows_in(vq, edge4, arrived, 20, 4)
        speed_in(s2, edge4, arrived, 24)
    k = 2 * block

    def after(t, mine):
        def act(n, r, core, total, seen):
            if n == 0:
                return None
            if mine:
                add_image(g, r, core * seen[0], first_block and t == 0)
            return added[k + t, r - 4]

        return act

    half = 8 + 8 * high
    field_step((up, uq), (vp, vq), 4 + 20 * high, 4, s2, weights, after(0, False))
    field_step((up, uq), (vp, vq), 8 + 4 * high, 12, s2, weights, after(0, True))
    add_source(info, source, wave, k, vp, 4 + 8 * high, 16)
    field_step((vp, vq), (None if last_block else up, uq), half, 8, s2, weights, after(1, True))
    if not last_block:
        add_source(info, source, wave, k + 1, up, half, 8)
        rows_back(outs[0], 0, up, half)
        rows_back(outs[0], 8, uq, half)


def far_p_kernel(block, blocks, n_in, *refs):
    first_block, last_block = block == 0, block == blocks - 1
    info, wave, source, weights, arrived = refs[:5]
    s2 = refs[7]
    outs = list(refs[n_in:])
    u, v = outs.pop(0), outs.pop(0)
    if first_block:
        s2 = outs.pop(0)
    lap = outs.pop(0)
    ext = u.shape[0]
    high = info[1]
    edge4 = 4 + high * (ext - 12)
    rows_in(u, high * (ext - 8), arrived, 0, 8)
    if first_block:
        rows_in(v, edge4, arrived, 8, 4)
        speed_in(s2, edge4, arrived, 12)
    k = 2 * block
    half = 8 + 8 * high

    def after(t, begin):
        def act(n, r, core, total, seen):
            lap[t, r - begin] = total

        return act

    begin = 4 + 16 * high
    field_step((u,), (v,), begin, 8, s2, weights, after(0, begin))
    add_source(info, source, wave, k, v, begin, 8)
    field_step((v,), (None if last_block else u,), half, 8, s2, weights, after(1, half))
    if not last_block:
        add_source(info, source, wave, k + 1, u, half, 8)
        rows_back(outs[0], 0, u, half)


def far_q_kernel(block, blocks, n_in, *refs):
    first_block, last_block = block == 0, block == blocks - 1
    info, added, weights, arrived, _, _, s2, lap = refs[:8]
    outs = list(refs[n_in:])
    u, v, g = outs.pop(0), outs.pop(0), outs.pop(0)
    ext, ny = u.shape[0], u.shape[1] - 2 * PAD
    own = ext - 2 * HALO
    high = info[1]
    rows_in(u, high * (ext - 8), arrived, 0, 8)
    if first_block:
        rows_in(v, 4 + high * (ext - 12), arrived, 8, 4)
    k = 2 * block
    half = 8 + 8 * high
    begin = 4 + 16 * high

    def after(t, low, mine):
        def act(n, r, core, total, seen):
            if mine:
                add_image(g, r, core * lap[t, r - low], first_block and t == 0)
            return added[k + t, r - 4]

        return act

    field_step((u,), (v,), 4 + 20 * high, 4, s2, weights, after(0, begin, False))
    field_step((u,), (v,), 8 + 12 * high, 4, s2, weights, after(0, begin, True))
    field_step((v,), (u,), half, 8, s2, weights, after(1, half, True))
    if last_block:
        final, sem = outs
        done = pltpu.make_async_copy(u.at[pl.ds(HALO, own), pl.ds(PAD, ny)], final.at[0], sem)
        done.start()
        done.wait()
    else:
        rows_back(outs[0], 0, u, half)


def call(kernel, block, blocks, scalars, args, outs, specs, alias, scratch=()):
    n_in = len(scalars) + len(args)
    return list(
        pl.pallas_call(
            functools.partial(kernel, block, blocks, n_in),
            out_shape=tuple(outs),
            in_specs=[SM] * len(scalars) + [VM] * len(args),
            out_specs=tuple(specs),
            scratch_shapes=list(scratch),
            input_output_aliases=alias,
            compiler_params=params(16),
            cost_estimate=cost(3.0),
        )(*scalars, *[keep(a) for a in args])
    )


def near_side(block, blocks, scalars, added, weights, arrived, fields, s2, g, shape):
    ext, ny, nz = s2.shape
    outs, alias = [on_chip(*fields[0].shape)] * 4, {6: 0, 7: 1, 8: 2, 9: 3}
    args = [added, weights, arrived, *fields, s2]
    if block == 0:
        alias[10] = 4
        outs.append(on_chip(ext, ny, nz))
    else:
        alias[11] = 4
        args.append(g)
    outs.append(on_chip(*shape))
    if block < blocks - 1:
        outs.append(on_chip(16, ny, nz))
    res = call(near_kernel, block, blocks, scalars, args, outs, [VM] * len(outs), alias)
    fields = res[:4]
    if block == 0:
        s2 = res.pop(4)
    return fields, s2, res[4], res[5:]


def far_p(block, blocks, scalars, weights, arrived, u, v, s2):
    ext, ny, nz = s2.shape
    outs, alias = [on_chip(*u.shape)] * 2, {5: 0, 6: 1}
    if block == 0:
        alias[7] = 2
        outs.append(on_chip(ext, ny, nz))
    outs.append(on_chip(2, 8, ny, nz))
    if block < blocks - 1:
        outs.append(on_chip(8, ny, nz))
    res = call(far_p_kernel, block, blocks, scalars, [weights, arrived, u, v, s2], outs, [VM] * len(outs), alias)
    if block == 0:
        s2 = res.pop(2)
    return res[0], res[1], s2, res[2], res[3:]


def far_q(block, blocks, info, added, weights, arrived, u, v, s2, lap, g):
    ext, ny, nz = s2.shape
    outs, specs = [on_chip(*u.shape)] * 2 + [on_chip(*g.shape)], [VM] * 3
    scratch = []
    if block < blocks - 1:
        outs.append(on_chip(8, ny, nz))
        specs.append(VM)
    else:
        outs.append(jax.ShapeDtypeStruct((1, ext - 2 * HALO, ny, nz), F32))
        specs.append(ANY)
        scratch.append(pltpu.SemaphoreType.DMA)
    args = [added, weights, arrived, u, v, s2, lap, g]
    return call(far_q_kernel, block, blocks, (info,), args, outs, specs, {4: 0, 5: 1, 8: 2}, scratch)


def swap_near(value, axis):
    return lax.ppermute(value, axis, [(i, i ^ 1) for i in range(lax.axis_size(axis))])


def swap_far(value, axis):
    count = lax.axis_size(axis)
    return lax.ppermute(value, axis, [(i, i + 1 if i % 2 else i - 1) for i in range(1, count - 1)])


def body(courant, p_current, p_later, q_current, q_later, wavelet, source_cell, receiver_cells, residual_data):
    rows = courant.shape[0]
    shots = lax.axis_size("shot")
    blocks = STEPS // 2
    index = lax.axis_index("space").astype(jnp.int32)
    info = jnp.stack([index * rows, index % 2])
    near, p_far = pack(info, p_current, p_later, q_current, q_later, courant)
    near = swap_near(near, "space")
    p_far = swap_far(p_far, "space")
    *fields, s2, added, weights, q_far = load(
        info, receiver_cells, residual_data, p_current, p_later, q_current, q_later, courant
    )
    q_far = swap_far(q_far, "space")
    scalars = (info, wavelet, source_cell)
    shape = (shots, rows, courant.shape[1] // shots, courant.shape[2])
    g = None
    for b in range(blocks):
        last = b == blocks - 1
        fields, s2, g, out = near_side(b, blocks, scalars, added, weights, near, fields, s2, g, shape)
        if not last:
            near = swap_near(out[0], "space")
        up, vp, uq, vq = fields
        up, vp, s2, lap, out = far_p(b, blocks, scalars, weights, p_far, up, vp, s2)
        if not last:
            p_far = swap_far(out[0], "space")
        uq, vq, g, out = far_q(b, blocks, info, added, weights, q_far, uq, vq, s2, lap, g)
        if not last:
            q_far = swap_far(out, "space")
        fields = [up, vp, uq, vq]
    arrived = lax.all_to_all(g, "shot", split_axis=0, concat_axis=0, tiled=True)
    gradient = arrived.sum(axis=0) * (1.0 / (SCALE * STEPS * shots))
    return gradient, out


def solution(mesh):
    in_specs = (
        P("space", None, None),
        P("shot", "space", None, None),
        P("shot", "space", None, None),
        P("shot", "space", None, None),
        P("shot", "space", None, None),
        P("shot", None),
        P("shot"),
        P("shot", None),
        P("shot", None, None),
    )
    out_specs = (P("space", "shot", None), P("shot", "space", None, None))
    return jax.shard_map(body, mesh=mesh, in_specs=in_specs, out_specs=out_specs, check_vma=False)
```

time: 90.1 us -> 85.1 us (0.945)
  the two profiles are of different devices: /device:TPU:322 before, /device:TPU:384 now
where the time goes in v2:
time: 85.1 us; the launch traced here: 84.3 us
  starting transfers between devices  33.8 us (40%)
  Pallas kernels  23.5 us (28%)
  blocking collectives  18.6 us (22%)
  waiting for transfers between devices  6.12 us (7%)
  between operations  1.54 us (2%)
    ppermute x6, starting transfers between devices, swap_far(): lax.ppermute(value, axis, [(i, i + 1 if i % 2 else i - 1) for i in range(...  22.7 us
    pallas_call x9, Pallas kernels, call(): pl.pallas_call(functools.partial(kernel, block, blocks, n_in), out_shape=...  19 us
    all_to_all x1, blocking collectives, body(): arrived = lax.all_to_all(g, 'shot', split_axis=0, concat_axis=0, tiled=True)  18.6 us
    ppermute x3, starting transfers between devices, swap_near(): lax.ppermute(value, axis, [(i, i ^ 1) for i in range(lax.axis_size(axis))])  11.1 us
    ppermute x6, waiting for transfers between devices, swap_far(): lax.ppermute(value, axis, [(i, i + 1 if i % 2 else i - 1) for i in range(...  6.11 us
    pallas_call x1, Pallas kernels, load(): pl.pallas_call(load_kernel, out_shape=(field,) * 4 + (on_chip(ext, ny, nz...  2.61 us
    pallas_call x1, Pallas kernels, pack(): pl.pallas_call(pack_kernel, out_shape=(on_chip(28, ny, nz), on_chip(16, n...  1.91 us
  transfers between devices with their start and end apart: 9, of which 3 were waited for; matrix products, arithmetic and copies ran while one was open for 0% of the time, Pallas kernels for 23%

profile of v2, /device:TPU:384, one launch (start us, length us, event | category | flops | bytes accessed | tf_op | source)
XLA Modules:
  0.0 84.3 jit_solution(13277241371480843976)
XLA Ops:
  0.7 1.9 %pack.1 = (f32[28,64,128]{2,1,0:T(8,128)S(1)}, f32[16,64,128]{2,1,0:T(8,128)S(1)}) custom-call(s32[2]{0:T(128)S(1)} %pad_add_fusion.info.refs_0_, f32[1,16,64,128]{3,2,1,0:T(8,128)} %pc.3, f32[1,16,64,128]{3,2,1,0:T(8,128)} %pn.3, f32[1,16,64,128]{3,2,1,0:T(8,128)} %qc.3, f32[1,16,64,128]{3,2,1,0:T(8,128)} %qn.3, f32[16,64,128]{2,1,0:T(8,128)} %speed.3), custom_call_target="tpu_custom_call" | custom-call | flops 4000000 | bytes 1048576 | tf_op jit(solution)/shard_map/pack/pallas_call | solution.py:68
  2.6 1.9 %collective-permute-start.1 = (f32[28,64,128]{2,1,0:T(8,128)S(1)}, f32[28,64,128]{2,1,0:T(8,128)S(1)}, u32[]{:S(2)}, u32[]{:S(2)}) collective-permute-start(f32[28,64,128]{2,1,0:T(8,128)S(1)} %get-tuple-element.53), channel_id=1, source_target_pairs={{0,8},{8,0},{16,24},{24,16},{32,40},{40,32},{48,56},{56,48},{64,72... | collective-permute-start | bytes 2752520 | tf_op jit(solution)/shard_map/ppermute | solution.py:457
  4.6 5.2 %collective-permute-start.2 = (f32[16,64,128]{2,1,0:T(8,128)S(1)}, f32[16,64,128]{2,1,0:T(8,128)S(1)}, u32[]{:S(2)}, u32[]{:S(2)}) collective-permute-start(f32[16,64,128]{2,1,0:T(8,128)S(1)} %get-tuple-element.61), channel_id=1, source_target_pairs={{8,16},{16,8},{24,32},{32,24},{40,48},{48,40},{56,64},{64,56},{72,... | collective-permute-start | bytes 1572872 | tf_op jit(solution)/shard_map/ppermute | solution.py:462
  10.4 2.6 %load.1 = (f32[32,80,128]{2,1,0:T(8,128)S(1)}, f32[32,80,128]{2,1,0:T(8,128)S(1)}, f32[32,80,128]{2,1,0:T(8,128)S(1)}, f32[32,80,128]{2,1,0:T(8,128)S(1)}, f32[3...) custom-call(s32[2]{0:T(128)S(1)} %pad_add_fusion.info.refs_0_, ...), custom_call_target="tpu_custom_call" | custom-call | flops 12000000 | bytes 1048576 | tf_op jit(solution)/shard_map/load/pallas_call | solution.py:149
  13.1 3.2 %shard_map.104 = (f32[32,80,128]{2,1,0:T(8,128)S(1)}, f32[32,80,128]{2,1,0:T(8,128)S(1)}, f32[32,80,128]{2,1,0:T(8,128)S(1)}, f32[32,80,128]{2,1,0:T(8,128)S(1)}...) custom-call(s32[2]{0:T(128)S(1)} %pad_add_fusion.info.refs_0_, ...), custom_call_target="tpu_custom_call", output_to_operand_aliasing={{0}: (6, {}), {1}: (7, {}), {2}: (8, {}), {3}: (9, {}), {4}... | custom-call | flops 12000000 | bytes 1048576 | tf_op jit(solution)/shard_map/pallas_call | solution.py:393
  16.2 1.9 %collective-permute-start.4 = (f32[16,64,128]{2,1,0:T(8,128)S(1)}, f32[16,64,128]{2,1,0:T(8,128)S(1)}, u32[]{:S(2)}, u32[]{:S(2)}) collective-permute-start(f32[16,64,128]{2,1,0:T(8,128)S(1)} %get-tuple-element.69), channel_id=1, source_target_pairs={{0,8},{8,0},{16,24},{24,16},{32,40},{40,32},{48,56},{56,48},{64,72... | collective-permute-start | bytes 1572872 | tf_op jit(solution)/shard_map/ppermute | solution.py:457
  18.2 2.5 %collective-permute-start = (f32[12,64,128]{2,1,0:T(8,128)S(1)}, f32[12,64,128]{2,1,0:T(8,128)S(1)}, u32[]{:S(2)}, u32[]{:S(2)}) collective-permute-start(f32[12,64,128]{2,1,0:T(8,128)S(1)} %get-tuple-element.52), channel_id=1, source_target_pairs={{8,16},{16,8},{24,32},{32,24},{40,48},{48,40},{56,64},{64,56},{72,... | collective-permute-start | bytes 1179656 | tf_op jit(solution)/shard_map/ppermute | solution.py:462
  20.7 1.5 %shard_map.105 = (f32[32,80,128]{2,1,0:T(8,128)S(1)}, f32[32,80,128]{2,1,0:T(8,128)S(1)}, f32[32,64,128]{2,1,0:T(8,128)S(1)}, f32[2,8,64,128]{3,2,1,0:T(8,128)S(1)}, f32[8,64,128]{2,1,0:T(8,128)S(1)}) custom-call(s32[2]{0:T(128)S(1)} %pad_add_fusion.info.refs_0_, f32[1,6]{1,0:T(1,128)S(1)} %copy-done, ...), custom_call_target="tpu_custom_call", output_to_operand_aliasing={{0}: (5, {}), {1}: (6, {}), {2}: (7, {})} | custom-call | flops 12000000 | bytes 1048576 | tf_op jit(solution)/shard_map/pallas_call | solution.py:393
  22.2 5.1 %collective-permute-start.5 = (f32[8,64,128]{2,1,0:T(8,128)S(1)}, f32[8,64,128]{2,1,0:T(8,128)S(1)}, u32[]{:S(2)}, u32[]{:S(2)}) collective-permute-start(f32[8,64,128]{2,1,0:T(8,128)S(1)} %get-tuple-element.77), channel_id=1, source_target_pairs={{8,16},{16,8},{24,32},{32,24},{40,48},{48,40},{56,64},{64,56},{72,... | collective-permute-start | bytes 786440 | tf_op jit(solution)/shard_map/ppermute | solution.py:462
  27.4 2.1 %collective-permute-done.refs_3_ = f32[12,64,128]{2,1,0:T(8,128)S(1)} collective-permute-done((f32[12,64,128]{2,1,0:T(8,128)S(1)}, f32[12,64,128]{2,1,0:T(8,128)S(1)}, u32[]{:S(2)}, u32[]{:S(2)}) %collective-permute-start) | collective-permute-done | bytes 393248 | tf_op jit(solution)/shard_map/ppermute | solution.py:462
  29.5 1.5 %shard_map.106 = (f32[32,80,128]{2,1,0:T(8,128)S(1)}, f32[32,80,128]{2,1,0:T(8,128)S(1)}, f32[8,16,8,128]{3,2,1,0:T(8,128)S(1)}, f32[8,64,128]{2,1,0:T(8,128)S(1)}) custom-call(s32[2]{0:T(128)S(1)} %pad_add_fusion.info.refs_0_, f32[6,24,64,128]{3,2,1,0:T(8,128)S(1)} %get-tuple-element.50.refs_3_.refs_1_, ...), custom_call_target="tpu_custom_call", output_to_operand_aliasing={{0}: (4, {}), {1}: (5, {}), {2}: (8, {})} | custom-call | flops 12000000 | bytes 1048576 | tf_op jit(solution)/shard_map/pallas_call | solution.py:393
  31.0 3.2 %shard_map.107 = (f32[32,80,128]{2,1,0:T(8,128)S(1)}, f32[32,80,128]{2,1,0:T(8,128)S(1)}, f32[32,80,128]{2,1,0:T(8,128)S(1)}, f32[32,80,128]{2,1,0:T(8,128)S(1)}...) custom-call(s32[2]{0:T(128)S(1)} %pad_add_fusion.info.refs_0_, ...), custom_call_target="tpu_custom_call", output_to_operand_aliasing={{0}: (6, {}), {1}: (7, {}), {2}: (8, {}), {3}: (9, {}), {4}... | custom-call | flops 12000000 | bytes 1048576 | tf_op jit(solution)/shard_map/pallas_call | solution.py:393
  34.2 7.2 %collective-permute-start.7 = (f32[16,64,128]{2,1,0:T(8,128)S(1)}, f32[16,64,128]{2,1,0:T(8,128)S(1)}, u32[]{:S(2)}, u32[]{:S(2)}) collective-permute-start(f32[16,64,128]{2,1,0:T(8,128)S(1)} %get-tuple-element.83), channel_id=1, source_target_pairs={{0,8},{8,0},{16,24},{24,16},{32,40},{40,32},{48,56},{56,48},{64,72... | collective-permute-start | bytes 1572872 | tf_op jit(solution)/shard_map/ppermute | solution.py:457
  41.4 2.2 %collective-permute-start.3 = (f32[8,64,128]{2,1,0:T(8,128)S(1)}, f32[8,64,128]{2,1,0:T(8,128)S(1)}, u32[]{:S(2)}, u32[]{:S(2)}) collective-permute-start(f32[8,64,128]{2,1,0:T(8,128)S(1)} %get-tuple-element.68), channel_id=1, source_target_pairs={{8,16},{16,8},{24,32},{32,24},{40,48},{48,40},{56,64},{64,56},{72,... | collective-permute-start | bytes 786440 | tf_op jit(solution)/shard_map/ppermute | solution.py:462
  43.6 1.4 %shard_map.108 = (f32[32,80,128]{2,1,0:T(8,128)S(1)}, f32[32,80,128]{2,1,0:T(8,128)S(1)}, f32[2,8,64,128]{3,2,1,0:T(8,128)S(1)}, f32[8,64,128]{2,1,0:T(8,128)S(1)}) custom-call(s32[2]{0:T(128)S(1)} %pad_add_fusion.info.refs_0_, f32[1,6]{1,0:T(1,128)S(1)} %copy-done, s32[1]{0:T(128)S(6)} %copy.74.refs_2_, ...), custom_call_target="tpu_custom_call", output_to_operand_aliasing={{0}: (5, {}), {1}: (6, {})} | custom-call | flops 12000000 | bytes 1048576 | tf_op jit(solution)/shard_map/pallas_call | solution.py:393
  45.1 5.5 %collective-permute-start.8 = (f32[8,64,128]{2,1,0:T(8,128)S(1)}, f32[8,64,128]{2,1,0:T(8,128)S(1)}, u32[]{:S(2)}, u32[]{:S(2)}) collective-permute-start(f32[8,64,128]{2,1,0:T(8,128)S(1)} %get-tuple-element.91), channel_id=1, source_target_pairs={{8,16},{16,8},{24,32},{32,24},{40,48},{48,40},{56,64},{64,56},{72,... | collective-permute-start | bytes 786440 | tf_op jit(solution)/shard_map/ppermute | solution.py:462
  50.5 0.8 collective-permute-done.3.refs_3_
  51.3 1.5 %shard_map.109 = (f32[32,80,128]{2,1,0:T(8,128)S(1)}, f32[32,80,128]{2,1,0:T(8,128)S(1)}, f32[8,16,8,128]{3,2,1,0:T(8,128)S(1)}, f32[8,64,128]{2,1,0:T(8,128)S(1)}) custom-call(s32[2]{0:T(128)S(1)} %pad_add_fusion.info.refs_0_, f32[6,24,64,128]{3,2,1,0:T(8,128)S(1)} %get-tuple-element.50.refs_3_.refs_1_, ...), custom_call_target="tpu_custom_call", output_to_operand_aliasing={{0}: (4, {}), {1}: (5, {}), {2}: (8, {})} | custom-call | flops 12000000 | bytes 1048576 | tf_op jit(solution)/shard_map/pallas_call | solution.py:393
  52.8 2.2 %collective-permute-start.6 = (f32[8,64,128]{2,1,0:T(8,128)S(1)}, f32[8,64,128]{2,1,0:T(8,128)S(1)}, u32[]{:S(2)}, u32[]{:S(2)}) collective-permute-start(f32[8,64,128]{2,1,0:T(8,128)S(1)} %get-tuple-element.82), channel_id=1, source_target_pairs={{8,16},{16,8},{24,32},{32,24},{40,48},{48,40},{56,64},{64,56},{72,... | collective-permute-start | bytes 786440 | tf_op jit(solution)/shard_map/ppermute | solution.py:462
  55.0 3.1 %shard_map.110 = (f32[32,80,128]{2,1,0:T(8,128)S(1)}, f32[32,80,128]{2,1,0:T(8,128)S(1)}, f32[32,80,128]{2,1,0:T(8,128)S(1)}, f32[32,80,128]{2,1,0:T(8,128)S(1)}, f32[8,16,8,128]{3,2,1,0:T(8,128)S(1)}) custom-call(s32[2]{0:T(128)S(1)} %pad_add_fusion.info.refs_0_, ...), custom_call_target="tpu_custom_call", output_to_operand_aliasing={{0}: (6, {}), {1}: (7, {}), {2}: (8, {}), {3}: (9, {}), {4}... | custom-call | flops 12000000 | bytes 1048576 | tf_op jit(solution)/shard_map/pallas_call | solution.py:393
  58.1 1.4 %shard_map.111 = (f32[32,80,128]{2,1,0:T(8,128)S(1)}, f32[32,80,128]{2,1,0:T(8,128)S(1)}, f32[2,8,64,128]{3,2,1,0:T(8,128)S(1)}) custom-call(s32[2]{0:T(128)S(1)} %pad_add_fusion.info.refs_0_, f32[1,6]{1,0:T(1,128)S(1)} %copy-done, s32[1]{0:T(128)S(6)} %copy.74.refs_2_, ...), custom_call_target="tpu_custom_call", output_to_operand_aliasing={{0}: (5, {}), {1}: (6, {})} | custom-call | flops 12000000 | bytes 1048576 | tf_op jit(solution)/shard_map/pallas_call | solution.py:393
  59.5 3.2 %collective-permute-done.6.refs_3_ = f32[8,64,128]{2,1,0:T(8,128)S(1)} collective-permute-done((f32[8,64,128]{2,1,0:T(8,128)S(1)}, f32[8,64,128]{2,1,0:T(8,128)S(1)}, u32[]{:S(2)}, u32[]{:S(2)}) %collective-permute-start.6) | collective-permute-done | bytes 262176 | tf_op jit(solution)/shard_map/ppermute | solution.py:462
  62.7 2.3 %shard_map.112 = (f32[32,80,128]{2,1,0:T(8,128)S(1)}, f32[32,80,128]{2,1,0:T(8,128)S(1)}, f32[8,16,8,128]{3,2,1,0:T(8,128)S(1)}, f32[1,16,64,128]{3,2,1,0:T(8,128)}) custom-call(s32[2]{0:T(128)S(1)} %pad_add_fusion.info.refs_0_, f32[6,24,64,128]{3,2,1,0:T(8,128)S(1)} %get-tuple-element.50.refs_3_.refs_1_, ...), custom_call_target="tpu_custom_call", output_to_operand_aliasing={{0}: (4, {}), {1}: (5, {}), {2}: (8, {})} | custom-call | flops 12000000 | bytes 1048576 | tf_op jit(solution)/shard_map/pallas_call | solution.py:393
  65.0 18.6 %all_to_all.5 = f32[8,16,8,128]{3,2,1,0:T(8,128)S(1)} all-to-all(f32[8,16,8,128]{3,2,1,0:T(8,128)S(1)} %get-tuple-element.96), channel_id=1, replica_groups=mesh['space'=64,'shot'=8] {'shot'}, dimensions={0} | all-to-all | bytes 1048576 | tf_op jit(solution)/shard_map/all_to_all | solution.py:494
  (16 shorter events, 0.8 us)
Async XLA Ops:
  0.7 9.7 %copy-start.2 = (f32[1,6,256]{2,0,1:T(1,128)S(1)}, f32[1,6,256]{2,0,1:T(1,128)}, u32[]{:S(2)}) copy-start(f32[1,6,256]{2,0,1:T(1,128)} %param.17) | copy-start | bytes 18436
  0.7 9.7 %copy-start.1 = (s32[1,256]{1,0:T(1,128)S(1)}, s32[1,256]{1,0:T(1,128)}, u32[]{:S(2)}) copy-start(s32[1,256]{1,0:T(1,128)} %cells.1) | copy-start | bytes 3076
  2.6 10.4 %collective-permute-start.1 = (f32[28,64,128]{2,1,0:T(8,128)S(1)}, f32[28,64,128]{2,1,0:T(8,128)S(1)}, u32[]{:S(2)}, u32[]{:S(2)}) collective-permute-start(f32[28,64,128]{2,1,0:T(8,128)S(1)} %get-tuple-element.53), channel_id=1, source_target_pairs={{0,8},{8,0},{16,24},{24,16},{32,40},{40,32},{48,56},{56,48},{64,72... | collective-permute-start | bytes 2752520 | tf_op jit(solution)/shard_map/ppermute | solution.py:457
  4.6 16.2 %collective-permute-start.2 = (f32[16,64,128]{2,1,0:T(8,128)S(1)}, f32[16,64,128]{2,1,0:T(8,128)S(1)}, u32[]{:S(2)}, u32[]{:S(2)}) collective-permute-start(f32[16,64,128]{2,1,0:T(8,128)S(1)} %get-tuple-element.61), channel_id=1, source_target_pairs={{8,16},{16,8},{24,32},{32,24},{40,48},{48,40},{56,64},{64,56},{72,... | collective-permute-start | bytes 1572872 | tf_op jit(solution)/shard_map/ppermute | solution.py:462
  10.4 2.6 %copy-start = (f32[1,6]{1,0:T(1,128)S(1)}, f32[1,6]{1,0:T(1,128)}, u32[]{:S(2)}) copy-start(f32[1,6]{1,0:T(1,128)} %refs_1_.11) | copy-start | bytes 76
  16.2 14.7 %collective-permute-start.4 = (f32[16,64,128]{2,1,0:T(8,128)S(1)}, f32[16,64,128]{2,1,0:T(8,128)S(1)}, u32[]{:S(2)}, u32[]{:S(2)}) collective-permute-start(f32[16,64,128]{2,1,0:T(8,128)S(1)} %get-tuple-element.69), channel_id=1, source_target_pairs={{0,8},{8,0},{16,24},{24,16},{32,40},{40,32},{48,56},{56,48},{64,72... | collective-permute-start | bytes 1572872 | tf_op jit(solution)/shard_map/ppermute | solution.py:457
  18.2 11.3 %collective-permute-start = (f32[12,64,128]{2,1,0:T(8,128)S(1)}, f32[12,64,128]{2,1,0:T(8,128)S(1)}, u32[]{:S(2)}, u32[]{:S(2)}) collective-permute-start(f32[12,64,128]{2,1,0:T(8,128)S(1)} %get-tuple-element.52), channel_id=1, source_target_pairs={{8,16},{16,8},{24,32},{32,24},{40,48},{48,40},{56,64},{64,56},{72,... | collective-permute-start | bytes 1179656 | tf_op jit(solution)/shard_map/ppermute | solution.py:462
  22.2 21.4 %collective-permute-start.5 = (f32[8,64,128]{2,1,0:T(8,128)S(1)}, f32[8,64,128]{2,1,0:T(8,128)S(1)}, u32[]{:S(2)}, u32[]{:S(2)}) collective-permute-start(f32[8,64,128]{2,1,0:T(8,128)S(1)} %get-tuple-element.77), channel_id=1, source_target_pairs={{8,16},{16,8},{24,32},{32,24},{40,48},{48,40},{56,64},{64,56},{72,... | collective-permute-start | bytes 786440 | tf_op jit(solution)/shard_map/ppermute | solution.py:462
  34.2 20.8 %collective-permute-start.7 = (f32[16,64,128]{2,1,0:T(8,128)S(1)}, f32[16,64,128]{2,1,0:T(8,128)S(1)}, u32[]{:S(2)}, u32[]{:S(2)}) collective-permute-start(f32[16,64,128]{2,1,0:T(8,128)S(1)} %get-tuple-element.83), channel_id=1, source_target_pairs={{0,8},{8,0},{16,24},{24,16},{32,40},{40,32},{48,56},{56,48},{64,72... | collective-permute-start | bytes 1572872 | tf_op jit(solution)/shard_map/ppermute | solution.py:457
  41.4 9.9 %collective-permute-start.3 = (f32[8,64,128]{2,1,0:T(8,128)S(1)}, f32[8,64,128]{2,1,0:T(8,128)S(1)}, u32[]{:S(2)}, u32[]{:S(2)}) collective-permute-start(f32[8,64,128]{2,1,0:T(8,128)S(1)} %get-tuple-element.68), channel_id=1, source_target_pairs={{8,16},{16,8},{24,32},{32,24},{40,48},{48,40},{56,64},{64,56},{72,... | collective-permute-start | bytes 786440 | tf_op jit(solution)/shard_map/ppermute | solution.py:462
  45.1 13.0 %collective-permute-start.8 = (f32[8,64,128]{2,1,0:T(8,128)S(1)}, f32[8,64,128]{2,1,0:T(8,128)S(1)}, u32[]{:S(2)}, u32[]{:S(2)}) collective-permute-start(f32[8,64,128]{2,1,0:T(8,128)S(1)} %get-tuple-element.91), channel_id=1, source_target_pairs={{8,16},{16,8},{24,32},{32,24},{40,48},{48,40},{56,64},{64,56},{72,... | collective-permute-start | bytes 786440 | tf_op jit(solution)/shard_map/ppermute | solution.py:462
  52.8 9.9 %collective-permute-start.6 = (f32[8,64,128]{2,1,0:T(8,128)S(1)}, f32[8,64,128]{2,1,0:T(8,128)S(1)}, u32[]{:S(2)}, u32[]{:S(2)}) collective-permute-start(f32[8,64,128]{2,1,0:T(8,128)S(1)} %get-tuple-element.82), channel_id=1, source_target_pairs={{8,16},{16,8},{24,32},{32,24},{40,48},{48,40},{56,64},{64,56},{72,... | collective-permute-start | bytes 786440 | tf_op jit(solution)/shard_map/ppermute | solution.py:462
